TPU v7x, 32 devices: a whole 2x2x4 slice. The times are simulated.
32 devices in a mesh: layer: 8 (over y, x, core), dp: 4 (over z).
Axes of the slice: x: 2, y: 2, z: 4, core: 2. Of those that a mesh axis runs over, the one named last changes fastest.
Arguments:
- initial: float32 [256, 1024], P('dp'), may hold values from -6 to 6
- norm_gains: float32 [32, 1024], P('layer'), may hold values from 0.25 to 1.75
- first_weights: bfloat16 [32, 1024, 2048], P('layer'), may hold values from -0.1875 to 0.1875
- second_weights: bfloat16 [32, 2048, 1024], P('layer'), may hold values from -0.046875 to 0.046875
Outputs:
- layer_states: float32 [32, 256, 1024], P('layer', 'dp')
- residual_ratios: float32 [7], replicated
- coarse_defects_four: float32 [32, 256, 1024], P('layer', 'dp')
- coarse_defects_sixteen: float32 [32, 256, 1024], P('layer', 'dp')
All inputs are finite; a program needn't handle non-finite values.
Results may differ from a plain program's by a relative error of at most 0.02.
Values sent between devices are 32-bit elements; how exact they have to be, the bound alone decides.
A program may use at most 128 MiB of HBM per device.

v0:
```python
import jax
import jax.numpy as jnp
from jax import lax
from jax.sharding import PartitionSpec as P

epsilon = 1e-06


def shifted(block, axis, distance):
    devices = range(lax.axis_size(axis))
    route = [(i - distance, i) for i in devices if i - distance in devices]
    return lax.ppermute(block, axis, route)


def branch(row_block, weight_in, weight_out, gain_row):
    mean_square = jnp.mean(row_block * row_block, axis=-1, keepdims=True)
    normed = (row_block * lax.rsqrt(mean_square + epsilon) * gain_row).astype(jnp.bfloat16)
    hidden = jax.nn.gelu(
        jnp.dot(normed, weight_in, preferred_element_type=jnp.float32), approximate=True
    ).astype(jnp.bfloat16)
    return jnp.dot(hidden, weight_out, preferred_element_type=jnp.float32)


def local(initial, norm_gains, first_weights, second_weights):
    slot_count = first_weights.shape[0]
    sections = lax.axis_size("layer")
    layer_total = slot_count * sections
    norm_count = layer_total // 4 - 1
    first_point = lax.axis_index("layer") * slot_count
    points = first_point + jnp.arange(slot_count, dtype=jnp.int32) + 1
    spacings = (1, 4, 16)

    def shaped(flags, rank):
        return flags.reshape((slot_count,) + (1,) * (rank - 1))

    def previous(values, level_index):
        spacing = spacings[level_index]
        if spacing >= slot_count:
            portion = values
            distance = spacing // slot_count
        else:
            portion = values[slot_count - spacing :]
            distance = 1
        if level_index == 0:
            arrived = shifted(portion, "layer", distance)
        elif level_index == 1:
            arrived = shifted(portion, "layer", distance)
        else:
            arrived = shifted(portion, "layer", distance)
        if spacing < slot_count:
            arrived = jnp.concatenate([arrived, values[: slot_count - spacing]], axis=0)
        return arrived

    def incoming(values, level_index, anchor):
        arrived = previous(values, level_index)
        from_anchor = shaped(points - spacings[level_index] == 0, values.ndim)
        return jnp.where(from_anchor, anchor, arrived)

    def advance(before, level_index, active, right_side):
        factor = float(spacings[level_index])
        results = []
        for slot in range(slot_count):

            def advance_compute(values, source, slot=slot):
                return (
                    values
                    + factor
                    * branch(values, first_weights[slot], second_weights[slot], norm_gains[slot])
                    + source
                )

            def advance_unchanged(values, source):
                return values

            source = right_side[slot] if right_side is not None else jnp.zeros_like(before[slot])
            results.append(
                lax.cond(active[slot], advance_compute, advance_unchanged, before[slot], source)
            )
        return jnp.stack(results)

    def relaxation(current, level_index, residues, right_side, anchor):
        modulus = 4 * spacings[level_index]
        for residue in residues:
            before = incoming(current, level_index, anchor)
            active = points % modulus == residue
            current = jnp.where(
                shaped(active, 3), advance(before, level_index, active, right_side), current
            )
        return (current, None)

    def restrict(current, level_index, right_side, anchor):
        spacing = spacings[level_index]
        factor = float(spacing)
        wide_factor = float(4 * spacing)
        before = incoming(current, level_index, anchor)
        far_state = incoming(current, level_index + 1, anchor)
        active = points % (4 * spacing) == 0
        row_count = current.shape[1]
        coarse_list = []
        gap_list = []
        step_list = []
        for slot in range(slot_count):

            def restrict_compute(near, distant, held, source, slot=slot):
                update = branch(
                    jnp.concatenate([near, distant], axis=0),
                    first_weights[slot],
                    second_weights[slot],
                    norm_gains[slot],
                )
                near_term = update[:row_count]
                fine_value = near + factor * near_term + source
                coarse = fine_value - (distant + wide_factor * update[row_count:])
                gap = fine_value - held
                return (coarse, jnp.sum(gap * gap), jnp.sum(near_term * near_term))

            def restrict_unchanged(near, distant, held, source):
                nothing = jnp.zeros((), near.dtype)
                return (jnp.zeros_like(near), nothing, nothing)

            source = right_side[slot] if right_side is not None else jnp.zeros_like(before[slot])
            coarse, gap_sum, step_sum = lax.cond(
                active[slot],
                restrict_compute,
                restrict_unchanged,
                before[slot],
                far_state[slot],
                current[slot],
                source,
            )
            coarse_list.append(coarse)
            gap_list.append(gap_sum)
            step_list.append(step_sum)
        return (jnp.stack(coarse_list), jnp.stack(gap_list), jnp.stack(step_list))

    def defects(current, level_index, anchor):
        spacing = spacings[level_index]
        factor = float(spacing)
        before = incoming(current, level_index, anchor)
        stepped = []
        for slot in range(slot_count):
            stepped.append(
                before[slot]
                + factor
                * branch(before[slot], first_weights[slot], second_weights[slot], norm_gains[slot])
            )
        valid = shaped(points >= spacing, 3)
        return jnp.where(valid, current - jnp.stack(stepped), 0.0)

    def multigrid_cycle(anchor):
        current = jnp.broadcast_to(anchor, (slot_count,) + anchor.shape)
        current, unused = relaxation(current, 0, (1, 2, 3), None, anchor)
        current, unused = relaxation(current, 0, (0,), None, anchor)
        current, carried = relaxation(current, 0, (1, 2, 3), None, anchor)
        rhs_one, gap_sums, step_sums = restrict(current, 0, None, anchor)
        current, carried = relaxation(current, 1, (4, 8, 12), rhs_one, anchor)
        rhs_two, unused_gaps, unused_steps = restrict(current, 1, rhs_one, anchor)
        for coarse_step in range(1, layer_total // 16 + 1):
            active = points == 16 * coarse_step
            before = incoming(current, 2, anchor)
            current = jnp.where(shaped(active, 3), advance(before, 2, active, rhs_two), current)
        current, unused = relaxation(current, 1, (4, 8, 12), rhs_one, anchor)
        current, unused = relaxation(current, 0, (1, 2, 3), None, anchor)
        defects_four = defects(current, 1, anchor)
        defects_sixteen = defects(current, 2, anchor)
        return (current, gap_sums, step_sums, defects_four, defects_sixteen)

    portions = [initial]
    outcomes = [multigrid_cycle(portion) for portion in portions]
    layer_states = jnp.concatenate([outcome[0] for outcome in outcomes], axis=1)
    defects_four = jnp.concatenate([outcome[3] for outcome in outcomes], axis=1)
    defects_sixteen = jnp.concatenate([outcome[4] for outcome in outcomes], axis=1)
    gap_sums = outcomes[0][1]
    step_sums = outcomes[0][2]
    counted = (points % 4 == 0) & (points >= 8)
    entry_index = points // 4 - 2
    one_hot = (
        (jnp.arange(norm_count, dtype=jnp.int32)[None, :] == entry_index[:, None])
        & counted[:, None]
    ).astype(jnp.float32)
    gap_vector = jnp.sum(gap_sums[:, None] * one_hot, axis=0)
    step_vector = jnp.sum(step_sums[:, None] * one_hot, axis=0)
    gap_total, step_total = lax.psum((gap_vector, step_vector), ("layer", "dp"))
    residual_ratios = jnp.sqrt(gap_total / (step_total + epsilon))
    return (layer_states, residual_ratios, defects_four, defects_sixteen)


def solution(mesh):
    placed = (P("dp", None), P("layer", None), P("layer", None, None), P("layer", None, None))
    return jax.shard_map(
        local,
        mesh=mesh,
        in_specs=placed,
        out_specs=(P("layer", "dp", None), P(), P("layer", "dp", None), P("layer", "dp", None)),
        check_vma=False,
    )
```

profile of v0, /device:TPU:0, one launch (start us, length us, event | category | flops | bytes accessed | tf_op | source)
XLA Modules:
  0.0 630.6 jit_solution(3890911371175717501)
XLA Ops:
  8.8 6.1 conditional.80
  23.7 6.1 conditional.85
  40.4 7.1 %conditional.90 = (f32[1,64,1024]{2,1,0:T(8,128)S(1)}) conditional(s32[]{:T(128)} %bitcast.423, f32[64,1024]{1,0:T(8,128)S(1)} %get-tuple-element.2047, (f32[64,1024]{1,0:T(8,128)}, f32[4,1024]{1,0:T(4,128)}, bf16[4,1024,2048]{2,1,0:T(8,128)(2,1)}, bf16[4,2048,1024]{2,1,0:T(8,128)(2,1)}) %tuple.1721), branch_computations={%region_30.31_spmd, %region_31.33_spmd} | conditional | flops 538443840 | bytes 9450504 | solution.py:77
  59.9 6.9 %conditional.95 = (f32[1,64,1024]{2,1,0:T(8,128)}) conditional(s32[]{:T(128)} %bitcast.432, f32[64,1024]{1,0:T(8,128)} %get-tuple-element.2042, (f32[64,1024]{1,0:T(8,128)S(1)}, f32[4,1024]{1,0:T(4,128)}, bf16[4,1024,2048]{2,1,0:T(8,128)(2,1)}, bf16[4,2048,1024]{2,1,0:T(8,128)(2,1)}) %tuple.1726), branch_computations={%region_45.46_spmd, %region_46.48_spmd} | conditional | flops 538443840 | bytes 10499108 | solution.py:77
  60.7 6.0 fusion.579
  79.3 6.9 %conditional.96 = (f32[1,64,1024]{2,1,0:T(8,128)}) conditional(s32[]{:T(128)} %bitcast.398, f32[64,1024]{1,0:T(8,128)} %get-tuple-element.2037, (f32[64,1024]{1,0:T(8,128)S(1)}, f32[4,1024]{1,0:T(4,128)}, bf16[4,1024,2048]{2,1,0:T(8,128)(2,1)}, bf16[4,2048,1024]{2,1,0:T(8,128)(2,1)}) %tuple.1727), branch_computations={%region_48.49_spmd, %region_49.51_spmd} | conditional | flops 538443840 | bytes 10499108 | solution.py:77
  80.1 6.0 fusion.617
  88.3 6.6 %collective-permute-start.5 = (f32[1,64,1024]{2,1,0:T(8,128)S(1)}, f32[1,64,1024]{2,1,0:T(8,128)S(1)}, u32[]{:S(2)}, u32[]{:S(2)}) collective-permute-start(f32[1,64,1024]{2,1,0:T(8,128)S(1)} %slice.1541), channel_id=1, source_target_pairs={{0,4},{4,8},{8,12},{12,16},{16,20},{20,24},{24,28},{1,5},{5,9},{9,... | collective-permute-start | bytes 786440 | tf_op jit(solution)/shard_map/ppermute | solution.py:12
  100.5 6.9 %conditional.101 = (f32[1,64,1024]{2,1,0:T(8,128)}) conditional(s32[]{:T(128)} %bitcast.414, f32[64,1024]{1,0:T(8,128)} %get-tuple-element.2036, (f32[64,1024]{1,0:T(8,128)S(1)}, f32[4,1024]{1,0:T(4,128)}, bf16[4,1024,2048]{2,1,0:T(8,128)(2,1)}, bf16[4,2048,1024]{2,1,0:T(8,128)(2,1)}) %tuple.1732), branch_computations={%region_63.64_spmd, %region_64.66_spmd} | conditional | flops 538443840 | bytes 10499108 | solution.py:77
  101.4 6.0 fusion.807
  110.7 6.6 %collective-permute-start.6 = (f32[1,64,1024]{2,1,0:T(8,128)S(1)}, f32[1,64,1024]{2,1,0:T(8,128)S(1)}, u32[]{:S(2)}, u32[]{:S(2)}) collective-permute-start(f32[1,64,1024]{2,1,0:T(8,128)S(1)} %slice.1547), channel_id=1, source_target_pairs={{0,4},{4,8},{8,12},{12,16},{16,20},{20,24},{24,28},{1,5},{5,9},{9,... | collective-permute-start | bytes 786440 | tf_op jit(solution)/shard_map/ppermute | solution.py:12
  121.5 6.9 %conditional.106 = (f32[1,64,1024]{2,1,0:T(8,128)}) conditional(s32[]{:T(128)} %bitcast.423, f32[64,1024]{1,0:T(8,128)} %get-tuple-element.2031, (f32[64,1024]{1,0:T(8,128)S(1)}, f32[4,1024]{1,0:T(4,128)}, bf16[4,1024,2048]{2,1,0:T(8,128)(2,1)}, bf16[4,2048,1024]{2,1,0:T(8,128)(2,1)}) %tuple.1737), branch_computations={%region_78.79_spmd, %region_79.81_spmd} | conditional | flops 538443840 | bytes 10499108 | solution.py:77
  122.3 6.0 fusion.997
  133.0 6.6 %collective-permute-start.7 = (f32[4,64,1024]{2,1,0:T(8,128)S(1)}, f32[4,64,1024]{2,1,0:T(8,128)S(1)}, u32[]{:S(2)}, u32[]{:S(2)}) collective-permute-start(f32[4,64,1024]{2,1,0:T(8,128)S(1)} %maximum_select_fusion.13), channel_id=1, source_target_pairs={{0,4},{4,8},{8,12},{12,16},{16,20},{20,24},{24,28},{1,5},{5,9},{9,... | collective-permute-start | bytes 3145736 | tf_op jit(solution)/shard_map/ppermute | solution.py:12
  151.9 11.8 %conditional.114 = (f32[64,1024]{1,0:T(8,128)}, f32[]{:T(128)}, f32[]{:T(128)}) conditional(s32[]{:T(128)} %bitcast.432, () %tuple.1253, (f32[4,64,1024]{2,1,0:T(8,128)}, f32[64,1024]{1,0:T(8,128)S(1)}, f32[4,1024]{1,0:T(4,128)S(1)}, bf16[4,1024,2048]{2,1,0:T(8,128)(2,1)}, bf16[4,2048,1024]{2,1,0:T(8,128)(2,1)}, ...), branch_computations={%region_108.109_spmd, %region_109.0_spmd} | conditional | flops 1077608576 | bytes 14170200 | solution.py:122
  153.7 6.0 fusion.1310
  163.7 7.2 %conditional.115 = (f32[1,64,1024]{2,1,0:T(8,128)}) conditional(s32[]{:T(128)} %bitcast.451, f32[64,1024]{1,0:T(8,128)} %copy-done.7, (f32[64,1024]{1,0:T(8,128)}, f32[4,1024]{1,0:T(4,128)S(1)}, bf16[4,1024,2048]{2,1,0:T(8,128)(2,1)}, bf16[4,2048,1024]{2,1,0:T(8,128)(2,1)}, f32[64,1024]{1,0:T(8,128)}) %tuple.1801), branch_computations={%region_113.114_spmd, %region_114.116_spmd} | conditional | flops 538574912 | bytes 9712648 | solution.py:77
  164.9 6.1 fusion.1363
  191.4 19.7 %collective-permute-start.10 = (f32[4,64,1024]{2,1,0:T(8,128)S(1)}, f32[4,64,1024]{2,1,0:T(8,128)S(1)}, u32[]{:S(2)}, u32[]{:S(2)}) collective-permute-start(f32[4,64,1024]{2,1,0:T(8,128)S(1)} %maximum_select_fusion.16), channel_id=1, source_target_pairs={{0,4},{4,8},{8,12},{12,16},{16,20},{20,24},{24,28},{1,5},{5,9},{9,... | collective-permute-start | bytes 3145736 | tf_op jit(solution)/shard_map/ppermute | solution.py:12
  223.0 10.4 %collective-permute-start.12 = (f32[4,64,1024]{2,1,0:T(8,128)S(1)}, f32[4,64,1024]{2,1,0:T(8,128)S(1)}, u32[]{:S(2)}, u32[]{:S(2)}) collective-permute-start(f32[4,64,1024]{2,1,0:T(8,128)S(1)} %maximum_select_fusion.17), channel_id=1, source_target_pairs={{0,4},{4,8},{8,12},{12,16},{16,20},{20,24},{24,28},{1,5},{5,9},{9,... | collective-permute-start | bytes 3145736 | tf_op jit(solution)/shard_map/ppermute | solution.py:12
  233.4 16.2 %collective-permute-start.11 = (f32[4,64,1024]{2,1,0:T(8,128)S(1)}, f32[4,64,1024]{2,1,0:T(8,128)S(1)}, u32[]{:S(2)}, u32[]{:S(2)}) collective-permute-start(f32[4,64,1024]{2,1,0:T(8,128)S(1)} %maximum_select_fusion.17), channel_id=1, source_target_pairs={{0,16},{4,20},{8,24},{12,28},{1,17},{5,21},{9,25},{13,29},{2,18},{... | collective-permute-start | bytes 3145736 | tf_op jit(solution)/shard_map/ppermute | solution.py:12
  255.8 26.8 %collective-permute-done.11 = f32[4,64,1024]{2,1,0:T(8,128)S(1)} collective-permute-done((f32[4,64,1024]{2,1,0:T(8,128)S(1)}, f32[4,64,1024]{2,1,0:T(8,128)S(1)}, u32[]{:S(2)}, u32[]{:S(2)}) %collective-permute-start.11) | collective-permute-done | bytes 1048608 | tf_op jit(solution)/shard_map/ppermute | solution.py:12
  302.1 19.3 %collective-permute-done.13 = f32[4,64,1024]{2,1,0:T(8,128)S(1)} collective-permute-done((f32[4,64,1024]{2,1,0:T(8,128)S(1)}, f32[4,64,1024]{2,1,0:T(8,128)S(1)}, u32[]{:S(2)}, u32[]{:S(2)}) %collective-permute-start.13) | collective-permute-done | bytes 1048608 | tf_op jit(solution)/shard_map/ppermute | solution.py:12
  336.3 6.9 %conditional.139 = (f32[1,64,1024]{2,1,0:T(8,128)}) conditional(s32[]{:T(128)} %bitcast.451, f32[64,1024]{1,0:T(8,128)} %get-tuple-element.2006, (f32[64,1024]{1,0:T(8,128)S(1)}, f32[4,1024]{1,0:T(4,128)S(1)}, bf16[4,1024,2048]{2,1,0:T(8,128)(2,1)}, bf16[4,2048,1024]{2,1,0:T(8,128)(2,1)}, f32[64,1024]{1,0:T(8,128)}) %tuple.1828), branch_computations={%region_185.186_spmd, %region_186.188_spmd} | conditional | flops 538574912 | bytes 10761252 | solution.py:77
  337.1 6.1 fusion.2395
  368.4 20.8 %collective-permute-start.16 = (f32[4,64,1024]{2,1,0:T(8,128)S(1)}, f32[4,64,1024]{2,1,0:T(8,128)S(1)}, u32[]{:S(2)}, u32[]{:S(2)}) collective-permute-start(f32[4,64,1024]{2,1,0:T(8,128)S(1)} %maximum_select_fusion.21), channel_id=1, source_target_pairs={{0,4},{4,8},{8,12},{12,16},{16,20},{20,24},{24,28},{1,5},{5,9},{9,... | collective-permute-start | bytes 3145736 | tf_op jit(solution)/shard_map/ppermute | solution.py:12
  396.7 5.9 maximum_select_fusion.22
  402.6 11.4 %collective-permute-start.17 = (f32[1,64,1024]{2,1,0:T(8,128)S(1)}, f32[1,64,1024]{2,1,0:T(8,128)S(1)}, u32[]{:S(2)}, u32[]{:S(2)}) collective-permute-start(f32[1,64,1024]{2,1,0:T(8,128)S(1)} %slice.1587), channel_id=1, source_target_pairs={{0,4},{4,8},{8,12},{12,16},{16,20},{20,24},{24,28},{1,5},{5,9},{9,... | collective-permute-start | bytes 786440 | tf_op jit(solution)/shard_map/ppermute | solution.py:12
  420.2 6.8 %conditional.148 = (f32[1,64,1024]{2,1,0:T(8,128)}) conditional(s32[]{:T(128)} %bitcast.398, f32[64,1024]{1,0:T(8,128)} %get-tuple-element.1993, (f32[64,1024]{1,0:T(8,128)S(1)}, f32[4,1024]{1,0:T(4,128)S(1)}, bf16[4,1024,2048]{2,1,0:T(8,128)(2,1)}, bf16[4,2048,1024]{2,1,0:T(8,128)(2,1)}) %tuple.1843), branch_computations={%region_212.213_spmd, %region_213.215_spmd} | conditional | flops 538443840 | bytes 10499108 | solution.py:77
  421.0 6.0 fusion.2785
  432.7 13.5 %collective-permute-start.18 = (f32[1,64,1024]{2,1,0:T(8,128)S(1)}, f32[1,64,1024]{2,1,0:T(8,128)S(1)}, u32[]{:S(2)}, u32[]{:S(2)}) collective-permute-start(f32[1,64,1024]{2,1,0:T(8,128)S(1)} %slice.1593), channel_id=1, source_target_pairs={{0,4},{4,8},{8,12},{12,16},{16,20},{20,24},{24,28},{1,5},{5,9},{9,... | collective-permute-start | bytes 786440 | tf_op jit(solution)/shard_map/ppermute | solution.py:12
  451.6 6.8 %conditional.153 = (f32[1,64,1024]{2,1,0:T(8,128)}) conditional(s32[]{:T(128)} %bitcast.414, f32[64,1024]{1,0:T(8,128)} %get-tuple-element.1992, (f32[64,1024]{1,0:T(8,128)S(1)}, f32[4,1024]{1,0:T(4,128)S(1)}, bf16[4,1024,2048]{2,1,0:T(8,128)(2,1)}, bf16[4,2048,1024]{2,1,0:T(8,128)(2,1)}) %tuple.1846), branch_computations={%region_227.228_spmd, %region_228.230_spmd} | conditional | flops 538443840 | bytes 10499108 | solution.py:77
  452.5 6.0 fusion.2975
  465.4 6.6 %collective-permute-start.19 = (f32[1,64,1024]{2,1,0:T(8,128)S(1)}, f32[1,64,1024]{2,1,0:T(8,128)S(1)}, u32[]{:S(2)}, u32[]{:S(2)}) collective-permute-start(f32[1,64,1024]{2,1,0:T(8,128)S(1)} %slice.1599), channel_id=1, source_target_pairs={{0,4},{4,8},{8,12},{12,16},{16,20},{20,24},{24,28},{1,5},{5,9},{9,... | collective-permute-start | bytes 786440 | tf_op jit(solution)/shard_map/ppermute | solution.py:12
  476.2 6.8 %conditional.158 = (f32[1,64,1024]{2,1,0:T(8,128)}) conditional(s32[]{:T(128)} %bitcast.423, f32[64,1024]{1,0:T(8,128)} %get-tuple-element.1987, (f32[64,1024]{1,0:T(8,128)S(1)}, f32[4,1024]{1,0:T(4,128)S(1)}, bf16[4,1024,2048]{2,1,0:T(8,128)(2,1)}, bf16[4,2048,1024]{2,1,0:T(8,128)(2,1)}) %tuple.1849), branch_computations={%region_242.243_spmd, %region_243.245_spmd} | conditional | flops 538443840 | bytes 10499108 | solution.py:77
  477.0 6.0 fusion.3165
  484.9 7.0 %maximum_select_fusion.28 = f32[4,64,1024]{2,1,0:T(8,128)} fusion(f32[1,64,1024]{2,1,0:T(8,128)} %get-tuple-element.1958, f32[1,64,1024]{2,1,0:T(8,128)} %get-tuple-element.1957, f32[1,64,1024]{2,1,0:T(8,128)} %get-tuple-element.1956, f32[1,64,1024]{2,1,0:T(8,128)} %get-tuple-element.1955, pred[4]{0:T(512)(128)(4,1)S(1)} %get-tuple-element.2112, ...), kind=kLoop, calls=%fused_computation.2628 | loop fusion | flops 18874368 | bytes 20185124 | tf_op jit(solution)/shard_map/jit(_where)/select_n | solution.py:86
  491.9 14.2 %collective-permute-start.21 = (f32[4,64,1024]{2,1,0:T(8,128)}, f32[4,64,1024]{2,1,0:T(8,128)}, u32[]{:S(2)}, u32[]{:S(2)}) collective-permute-start(f32[4,64,1024]{2,1,0:T(8,128)} %maximum_select_fusion.28), channel_id=1, source_target_pairs={{0,16},{4,20},{8,24},{12,28},{1,17},{5,21},{9,25},{13,29},{2,18},{... | collective-permute-start | bytes 3145736 | tf_op jit(solution)/shard_map/ppermute | solution.py:12
  508.8 61.7 %all-reduce = (f32[7]{0:T(128)S(1)}, f32[7]{0:T(128)S(1)}) all-reduce(f32[7]{0:T(128)S(1)} %get-tuple-element.1976, f32[7]{0:T(128)S(1)} %get-tuple-element.1975), channel_id=1, replica_groups=mesh['layer'=8,'dp'=4] {'layer','dp'}, use_global_device_ids=true, to_apply=%region_249.250 | all-reduce | flops 14 | bytes 112 | tf_op jit(solution)/shard_map/psum | solution.py:183
  574.2 6.0 fusion.3349
  580.2 6.0 fusion.3340
  586.2 6.0 fusion.3331
  592.2 6.0 fusion.3322
  598.2 6.0 fusion.3313
  604.2 6.0 fusion.3304
  610.2 6.0 fusion.3295
  616.2 6.0 fusion.3286
  622.2 7.9 %fusion.3353 = (f32[4,64,1024]{2,1,0:T(8,128)}, f32[4,64,1024]{2,1,0:T(8,128)}) fusion(f32[1,64,1024]{2,1,0:T(8,128)} %fusion.3349, f32[1,64,1024]{2,1,0:T(8,128)} %fusion.3331, f32[1,64,1024]{2,1,0:T(8,128)} %fusion.3313, f32[1,64,1024]{2,1,0:T(8,128)} %fusion.3295, pred[4]{0:T(512)(128)(4,1)S(1)} %get-tuple-element.2108, f32[1,64,1024]{2,1,0:T(8,128)} %fusion.3340, ...), kind=kLoop, calls=%fused_computation.2632 | loop fusion | flops 21495808 | bytes 23330860 | tf_op jit(solution)/shard_map/jit(_where)/select_n | solution.py:148
  (409 shorter events, 236.6 us)
Async XLA Ops:
  0.6 5.7 collective-permute-start
  6.3 141.3 %copy-start.77 = (pred[4]{0:T(512)(128)(4,1)}, pred[4]{0:T(512)(128)(4,1)S(1)}, u32[]{:S(2)}) copy-start(pred[4]{0:T(512)(128)(4,1)S(1)} %fusion.3563) | copy-start | bytes 16
  8.7 6.2 copy-start
  15.2 8.1 %collective-permute-start.1 = (f32[1,64,1024]{2,1,0:T(8,128)S(1)}, f32[1,64,1024]{2,1,0:T(8,128)S(1)}, u32[]{:S(2)}, u32[]{:S(2)}) collective-permute-start(f32[1,64,1024]{2,1,0:T(8,128)S(1)} %slice.1517), channel_id=1, source_target_pairs={{0,4},{4,8},{8,12},{12,16},{16,20},{20,24},{24,28},{1,5},{5,9},{9,... | collective-permute-start | bytes 786440 | tf_op jit(solution)/shard_map/ppermute | solution.py:12
  30.4 7.6 %collective-permute-start.2 = (f32[1,64,1024]{2,1,0:T(8,128)S(1)}, f32[1,64,1024]{2,1,0:T(8,128)S(1)}, u32[]{:S(2)}, u32[]{:S(2)}) collective-permute-start(f32[1,64,1024]{2,1,0:T(8,128)S(1)} %slice.1523), channel_id=1, source_target_pairs={{0,4},{4,8},{8,12},{12,16},{16,20},{20,24},{24,28},{1,5},{5,9},{9,... | collective-permute-start | bytes 786440 | tf_op jit(solution)/shard_map/ppermute | solution.py:12
  48.0 7.7 %collective-permute-start.3 = (f32[1,64,1024]{2,1,0:T(8,128)S(1)}, f32[1,64,1024]{2,1,0:T(8,128)S(1)}, u32[]{:S(2)}, u32[]{:S(2)}) collective-permute-start(f32[1,64,1024]{2,1,0:T(8,128)S(1)} %slice.1529), channel_id=1, source_target_pairs={{0,4},{4,8},{8,12},{12,16},{16,20},{20,24},{24,28},{1,5},{5,9},{9,... | collective-permute-start | bytes 786440 | tf_op jit(solution)/shard_map/ppermute | solution.py:12
  56.6 2.5 copy-start.1
  56.7 3.2 copy-start.2
  56.7 3.2 copy-start.3
  68.7 5.5 collective-permute-start.4
  88.3 7.7 %collective-permute-start.5 = (f32[1,64,1024]{2,1,0:T(8,128)S(1)}, f32[1,64,1024]{2,1,0:T(8,128)S(1)}, u32[]{:S(2)}, u32[]{:S(2)}) collective-permute-start(f32[1,64,1024]{2,1,0:T(8,128)S(1)} %slice.1541), channel_id=1, source_target_pairs={{0,4},{4,8},{8,12},{12,16},{16,20},{20,24},{24,28},{1,5},{5,9},{9,... | collective-permute-start | bytes 786440 | tf_op jit(solution)/shard_map/ppermute | solution.py:12
  110.7 7.7 %collective-permute-start.6 = (f32[1,64,1024]{2,1,0:T(8,128)S(1)}, f32[1,64,1024]{2,1,0:T(8,128)S(1)}, u32[]{:S(2)}, u32[]{:S(2)}) collective-permute-start(f32[1,64,1024]{2,1,0:T(8,128)S(1)} %slice.1547), channel_id=1, source_target_pairs={{0,4},{4,8},{8,12},{12,16},{16,20},{20,24},{24,28},{1,5},{5,9},{9,... | collective-permute-start | bytes 786440 | tf_op jit(solution)/shard_map/ppermute | solution.py:12
  130.2 21.7 %copy-start.24 = (f32[4,1024]{1,0:T(4,128)S(1)}, f32[4,1024]{1,0:T(4,128)}, u32[]{:S(2)}) copy-start(f32[4,1024]{1,0:T(4,128)} %param.165) | copy-start | bytes 49156
  133.0 14.5 %copy-start.23 = (f32[4,64,1024]{2,1,0:T(8,128)}, f32[4,64,1024]{2,1,0:T(8,128)S(1)}, u32[]{:S(2)}) copy-start(f32[4,64,1024]{2,1,0:T(8,128)S(1)} %maximum_select_fusion.13) | copy-start | bytes 3145732
  133.0 14.6 %collective-permute-start.7 = (f32[4,64,1024]{2,1,0:T(8,128)S(1)}, f32[4,64,1024]{2,1,0:T(8,128)S(1)}, u32[]{:S(2)}, u32[]{:S(2)}) collective-permute-start(f32[4,64,1024]{2,1,0:T(8,128)S(1)} %maximum_select_fusion.13), channel_id=1, source_target_pairs={{0,4},{4,8},{8,12},{12,16},{16,20},{20,24},{24,28},{1,5},{5,9},{9,... | collective-permute-start | bytes 3145736 | tf_op jit(solution)/shard_map/ppermute | solution.py:12
  139.6 8.0 %copy-start.76 = (f32[1,64,1024]{2,1,0:T(8,128)}, f32[1,64,1024]{2,1,0:T(8,128)S(1)}, u32[]{:S(2)}) copy-start(f32[1,64,1024]{2,1,0:T(8,128)S(1)} %slice.1554) | copy-start | bytes 786436
  139.6 7.9 %collective-permute-start.8 = (f32[1,64,1024]{2,1,0:T(8,128)S(1)}, f32[1,64,1024]{2,1,0:T(8,128)S(1)}, u32[]{:S(2)}, u32[]{:S(2)}) collective-permute-start(f32[1,64,1024]{2,1,0:T(8,128)S(1)} %slice.1554), channel_id=1, source_target_pairs={{0,4},{4,8},{8,12},{12,16},{16,20},{20,24},{24,28},{1,5},{5,9},{9,... | collective-permute-start | bytes 786440 | tf_op jit(solution)/shard_map/ppermute | solution.py:12
  149.0 2.2 copy-start.4
  149.0 2.9 copy-start.5
  149.0 2.9 copy-start.6
  149.0 2.9 copy-start.7
  176.6 7.0 %collective-permute-start.9 = (f32[4,64,1024]{2,1,0:T(8,128)S(1)}, f32[4,64,1024]{2,1,0:T(8,128)S(1)}, u32[]{:S(2)}, u32[]{:S(2)}) collective-permute-start(f32[4,64,1024]{2,1,0:T(8,128)S(1)} %maximum_select_fusion.15), channel_id=1, source_target_pairs={{0,4},{4,8},{8,12},{12,16},{16,20},{20,24},{24,28},{1,5},{5,9},{9,... | collective-permute-start | bytes 3145736 | tf_op jit(solution)/shard_map/ppermute | solution.py:12
  184.5 2.5 copy-start.14
  184.5 3.2 copy-start.15
  184.5 3.2 copy-start.16
  191.4 22.9 %collective-permute-start.10 = (f32[4,64,1024]{2,1,0:T(8,128)S(1)}, f32[4,64,1024]{2,1,0:T(8,128)S(1)}, u32[]{:S(2)}, u32[]{:S(2)}) collective-permute-start(f32[4,64,1024]{2,1,0:T(8,128)S(1)} %maximum_select_fusion.16), channel_id=1, source_target_pairs={{0,4},{4,8},{8,12},{12,16},{16,20},{20,24},{24,28},{1,5},{5,9},{9,... | collective-permute-start | bytes 3145736 | tf_op jit(solution)/shard_map/ppermute | solution.py:12
  215.3 2.5 copy-start.17
  215.3 3.2 copy-start.18
  215.3 3.2 copy-start.19
  223.0 32.9 %collective-permute-start.12 = (f32[4,64,1024]{2,1,0:T(8,128)S(1)}, f32[4,64,1024]{2,1,0:T(8,128)S(1)}, u32[]{:S(2)}, u32[]{:S(2)}) collective-permute-start(f32[4,64,1024]{2,1,0:T(8,128)S(1)} %maximum_select_fusion.17), channel_id=1, source_target_pairs={{0,4},{4,8},{8,12},{12,16},{16,20},{20,24},{24,28},{1,5},{5,9},{9,... | collective-permute-start | bytes 3145736 | tf_op jit(solution)/shard_map/ppermute | solution.py:12
  233.4 49.3 %collective-permute-start.11 = (f32[4,64,1024]{2,1,0:T(8,128)S(1)}, f32[4,64,1024]{2,1,0:T(8,128)S(1)}, u32[]{:S(2)}, u32[]{:S(2)}) collective-permute-start(f32[4,64,1024]{2,1,0:T(8,128)S(1)} %maximum_select_fusion.17), channel_id=1, source_target_pairs={{0,16},{4,20},{8,24},{12,28},{1,17},{5,21},{9,25},{13,29},{2,18},{... | collective-permute-start | bytes 3145736 | tf_op jit(solution)/shard_map/ppermute | solution.py:12
  284.0 2.2 copy-start.9
  284.1 2.9 copy-start.10
  284.1 2.9 copy-start.11
  284.1 2.9 copy-start.12
  294.3 27.0 %collective-permute-start.13 = (f32[4,64,1024]{2,1,0:T(8,128)S(1)}, f32[4,64,1024]{2,1,0:T(8,128)S(1)}, u32[]{:S(2)}, u32[]{:S(2)}) collective-permute-start(f32[4,64,1024]{2,1,0:T(8,128)S(1)} %maximum_select_fusion.18), channel_id=1, source_target_pairs={{0,16},{4,20},{8,24},{12,28},{1,17},{5,21},{9,25},{13,29},{2,18},{... | collective-permute-start | bytes 3145736 | tf_op jit(solution)/shard_map/ppermute | solution.py:12
  322.3 2.5 copy-start.20
  322.3 3.2 copy-start.21
  322.3 3.2 copy-start.22
  330.6 3.6 collective-permute-start.14
  351.1 6.6 %collective-permute-start.15 = (f32[4,64,1024]{2,1,0:T(8,128)S(1)}, f32[4,64,1024]{2,1,0:T(8,128)S(1)}, u32[]{:S(2)}, u32[]{:S(2)}) collective-permute-start(f32[4,64,1024]{2,1,0:T(8,128)S(1)} %maximum_select_fusion.20), channel_id=1, source_target_pairs={{0,4},{4,8},{8,12},{12,16},{16,20},{20,24},{24,28},{1,5},{5,9},{9,... | collective-permute-start | bytes 3145736 | tf_op jit(solution)/shard_map/ppermute | solution.py:12
  368.4 23.0 %collective-permute-start.16 = (f32[4,64,1024]{2,1,0:T(8,128)S(1)}, f32[4,64,1024]{2,1,0:T(8,128)S(1)}, u32[]{:S(2)}, u32[]{:S(2)}) collective-permute-start(f32[4,64,1024]{2,1,0:T(8,128)S(1)} %maximum_select_fusion.21), channel_id=1, source_target_pairs={{0,4},{4,8},{8,12},{12,16},{16,20},{20,24},{24,28},{1,5},{5,9},{9,... | collective-permute-start | bytes 3145736 | tf_op jit(solution)/shard_map/ppermute | solution.py:12
  395.6 19.6 %copy-start.78 = (pred[4]{0:T(512)(128)(4,1)S(1)}, pred[4]{0:T(512)(128)(4,1)}, u32[]{:S(2)}) copy-start(pred[4]{0:T(512)(128)(4,1)} %copy-done.77) | copy-start | bytes 16
  402.6 12.5 %collective-permute-start.17 = (f32[1,64,1024]{2,1,0:T(8,128)S(1)}, f32[1,64,1024]{2,1,0:T(8,128)S(1)}, u32[]{:S(2)}, u32[]{:S(2)}) collective-permute-start(f32[1,64,1024]{2,1,0:T(8,128)S(1)} %slice.1587), channel_id=1, source_target_pairs={{0,4},{4,8},{8,12},{12,16},{16,20},{20,24},{24,28},{1,5},{5,9},{9,... | collective-permute-start | bytes 786440 | tf_op jit(solution)/shard_map/ppermute | solution.py:12
  432.7 14.6 %collective-permute-start.18 = (f32[1,64,1024]{2,1,0:T(8,128)S(1)}, f32[1,64,1024]{2,1,0:T(8,128)S(1)}, u32[]{:S(2)}, u32[]{:S(2)}) collective-permute-start(f32[1,64,1024]{2,1,0:T(8,128)S(1)} %slice.1593), channel_id=1, source_target_pairs={{0,4},{4,8},{8,12},{12,16},{16,20},{20,24},{24,28},{1,5},{5,9},{9,... | collective-permute-start | bytes 786440 | tf_op jit(solution)/shard_map/ppermute | solution.py:12
  465.4 7.7 %collective-permute-start.19 = (f32[1,64,1024]{2,1,0:T(8,128)S(1)}, f32[1,64,1024]{2,1,0:T(8,128)S(1)}, u32[]{:S(2)}, u32[]{:S(2)}) collective-permute-start(f32[1,64,1024]{2,1,0:T(8,128)S(1)} %slice.1599), channel_id=1, source_target_pairs={{0,4},{4,8},{8,12},{12,16},{16,20},{20,24},{24,28},{1,5},{5,9},{9,... | collective-permute-start | bytes 786440 | tf_op jit(solution)/shard_map/ppermute | solution.py:12
  491.9 79.1 %collective-permute-start.21 = (f32[4,64,1024]{2,1,0:T(8,128)}, f32[4,64,1024]{2,1,0:T(8,128)}, u32[]{:S(2)}, u32[]{:S(2)}) collective-permute-start(f32[4,64,1024]{2,1,0:T(8,128)} %maximum_select_fusion.28), channel_id=1, source_target_pairs={{0,16},{4,20},{8,24},{12,28},{1,17},{5,21},{9,25},{13,29},{2,18},{... | collective-permute-start | bytes 3145736 | tf_op jit(solution)/shard_map/ppermute | solution.py:12
  506.1 64.9 %collective-permute-start.20 = (f32[4,64,1024]{2,1,0:T(8,128)}, f32[4,64,1024]{2,1,0:T(8,128)}, u32[]{:S(2)}, u32[]{:S(2)}) collective-permute-start(f32[4,64,1024]{2,1,0:T(8,128)} %maximum_select_fusion.28), channel_id=1, source_target_pairs={{0,4},{4,8},{8,12},{12,16},{16,20},{20,24},{24,28},{1,5},{5,9},{9,... | collective-permute-start | bytes 3145736 | tf_op jit(solution)/shard_map/ppermute | solution.py:12
  (12 other events, 9.8 us)
where the time goes:
time: 641 us; the launch traced here: 631 us
  starting transfers between devices  174 us (27%)
  matrix products  124 us (19%)
  local copies, waits for them, and re-layouts  91.3 us (14%)
  other arithmetic  88.6 us (14%)
  blocking collectives  61.7 us (10%)
  waiting for transfers between devices  59.1 us (9%)
  between operations  28.2 us (4%)
    ppermute x22, starting transfers between devices, shifted(): return lax.ppermute(block, axis, route)  174 us
    dot_general x21, matrix products, branch(): return jnp.dot(hidden, weight_out, preferred_element_type=jnp.float32)  124 us
    psum x1, blocking collectives, local(): gap_total, step_total = lax.psum((gap_vector, step_vector), ('layer', 'dp'))  61.7 us
    ppermute x22, waiting for transfers between devices, shifted(): return lax.ppermute(block, axis, route)  59.1 us
    unnamed x128, local copies, waits for them, and re-layouts  56.1 us
    select_n x16, other arithmetic, relaxation(): jnp.where(shaped(active, 3), advance(before, level_index, active, right_s...  55.6 us
  transfers between devices with their start and end apart: 22, of which 11 were waited for; matrix products, arithmetic and copies ran while one was open for 1% of the time, Pallas kernels for 0%

commit v1 on v0

--- a/solution.py
+++ b/solution.py
@@ -185,10 +185,94 @@
     return (layer_states, residual_ratios, defects_four, defects_sixteen)
 
 
+def local_quads(initial, norm_gains, first_weights, second_weights):
+    sections = lax.axis_size("layer")
+    blocks = sections // 4
+    here = lax.axis_index("layer")
+    place = here % 4
+    rows = initial.shape[0]
+
+    def moved(slot, *states):
+        stacked = states[0] if len(states) == 1 else jnp.concatenate(states, axis=0)
+        return branch(stacked, first_weights[slot], second_weights[slot], norm_gains[slot])
+
+    def near(values):
+        return jnp.where(here == 0, initial, shifted(values, "layer", 1))
+
+    def distant(values):
+        return jnp.where(here == 3, initial, shifted(values, "layer", 4))
+
+    state = initial
+    for slot in range(4):
+        state = state + moved(slot, state)
+    point = state
+    left = near(point)
+    far = distant(point)
+    state = left
+    for slot in range(3):
+        state = state + moved(slot, state)
+    update = moved(3, state, left, far)
+    near_term = update[:rows]
+    fine = state + near_term
+    rhs_one = fine - (left + 4.0 * update[rows : 2 * rows])
+    far_step = far + 16.0 * update[2 * rows :]
+    gap = fine - point
+    gap_sum = jnp.sum(gap * gap)
+    step_sum = jnp.sum(near_term * near_term)
+
+    point = jnp.where(place == 0, fine, point)
+    for residue in (1, 2, 3):
+        before = near(point)
+        stepped = before + 4.0 * moved(3, before) + rhs_one
+        point = jnp.where(place == residue, stepped, point)
+    rhs_two = point - far_step
+
+    wide = place == 3
+    factor = jnp.where(wide, 16.0, 4.0)
+    source = jnp.where(wide, rhs_two, rhs_one)
+    for block in range(1, blocks):
+        before = jnp.where(wide, distant(point), near(point))
+        stepped = before + factor * moved(3, before) + source
+        point = jnp.where((here == 4 * block) | (here == 4 * block + 3), stepped, point)
+    for residue in (1, 2):
+        before = near(point)
+        stepped = before + 4.0 * moved(3, before) + rhs_one
+        point = jnp.where(place == residue, stepped, point)
+
+    left = near(point)
+    far = distant(point)
+    state = left
+    states = []
+    for slot in range(3):
+        state = state + moved(slot, state)
+        states.append(state)
+    states.append(point)
+    lefts = [shifted(s, "layer", 1) for s in states[:3]] + [left]
+    fars = [shifted(s, "layer", 4) for s in states[:3]] + [far]
+    fours = []
+    sixteens = []
+    for slot in range(4):
+        update = moved(slot, lefts[slot], fars[slot])
+        fours.append(states[slot] - (lefts[slot] + 4.0 * update[:rows]))
+        sixteens.append(states[slot] - (fars[slot] + 16.0 * update[rows:]))
+    points = here * 4 + jnp.arange(4, dtype=jnp.int32) + 1
+    defects_four = jnp.where((points >= 4)[:, None, None], jnp.stack(fours), 0.0)
+    defects_sixteen = jnp.where((points >= 16)[:, None, None], jnp.stack(sixteens), 0.0)
+    one_hot = (jnp.arange(sections - 1) == here - 1).astype(jnp.float32)
+    gap_total, step_total = lax.psum((gap_sum * one_hot, step_sum * one_hot), ("layer", "dp"))
+    ratios = jnp.sqrt(gap_total / (step_total + epsilon))
+    return (jnp.stack(states), ratios, defects_four, defects_sixteen)
+
+
+def chosen(initial, norm_gains, first_weights, second_weights):
+    quads = first_weights.shape[0] == 4 and lax.axis_size("layer") % 4 == 0
+    return (local_quads if quads else local)(initial, norm_gains, first_weights, second_weights)
+
+
 def solution(mesh):
     placed = (P("dp", None), P("layer", None), P("layer", None, None), P("layer", None, None))
     return jax.shard_map(
-        local,
+        chosen,
         mesh=mesh,
         in_specs=placed,
         out_specs=(P("layer", "dp", None), P(), P("layer", "dp", None), P("layer", "dp", None)),

time: 641 us -> 270 us (0.42); the launches traced: 631 us -> 269 us
  starting transfers between devices: 174 us -> 74.9 us
  local copies, waits for them, and re-layouts: 91.3 us -> 1.01 us
  other arithmetic: 88.6 us -> 11.6 us
  waiting for transfers between devices: 59.1 us -> 29.7 us
  between operations: 28.2 us -> 1.07 us
  blocking collectives: 61.7 us -> 39.5 us
  matrix products: 124 us -> 112 us
    ppermute x22 -> x17, starting transfers between devices: 174 us -> 74.9 us  [shifted(): return lax.ppermute(block, axis, route)]
    select_n x38 -> x1, other arithmetic: 81.1 us -> 1.58 us  [local_quads(): jnp.where((points >= 4)[:, None, None], jnp.stack(fours), 0.0)]
    unnamed x128 -> x7, local copies, waits for them, and re-layouts: 56.1 us -> 0.06 us
    ppermute x22 -> x17, waiting for transfers between devices: 59.1 us -> 29.7 us  [shifted(): return lax.ppermute(block, axis, route)]
    psum x1, blocking collectives: 61.7 us -> 39.5 us  [local_quads(): lax.psum((gap_sum * one_hot, step_sum * one_hot), ('layer', 'dp'))]
    squeeze x19 -> x0, local copies, waits for them, and re-layouts: 13.7 us -> none  [the longest x18 12.6 us: advance(): before[slot]]
    dot_general x21, matrix products: 124 us -> 112 us  [branch(): return jnp.dot(hidden, weight_out, preferred_element_type=jnp.float32)]
    slice x45 -> x1, local copies, waits for them, and re-layouts: 13.1 us -> 0.89 us  [moved(): norm_gains[slot]]
  transfers between devices with their start and end apart: 22 -> 17, of which waited for: 11 -> 10; matrix products, arithmetic and copies ran while one was open for 1% -> 4% of each run, Pallas kernels for 0% -> 0%
where the time goes in v1:
time: 270 us; the launch traced here: 269 us
  matrix products  112 us (41%)
  starting transfers between devices  74.9 us (28%)
  blocking collectives  39.5 us (15%)
  waiting for transfers between devices  29.7 us (11%)
  other arithmetic  11.6 us (4%)
    dot_general x21, matrix products, branch(): return jnp.dot(hidden, weight_out, preferred_element_type=jnp.float32)  112 us
    ppermute x17, starting transfers between devices, shifted(): return lax.ppermute(block, axis, route)  74.9 us
    psum x1, blocking collectives, local_quads(): lax.psum((gap_sum * one_hot, step_sum * one_hot), ('layer', 'dp'))  39.5 us
    ppermute x17, waiting for transfers between devices, shifted(): return lax.ppermute(block, axis, route)  29.7 us
  transfers between devices with their start and end apart: 17, of which 10 were waited for; matrix products, arithmetic and copies ran while one was open for 4% of the time, Pallas kernels for 0%

profile of v1, /device:TPU:0, one launch (start us, length us, event | category | flops | bytes accessed | tf_op | source)
XLA Modules:
  0.0 269.5 jit_solution(11445225732891216298)
XLA Ops:
  2.6 5.4 %multiply_reduce_fusion.21 = (f32[64]{0:T(128)S(1)}, f32[64,1024]{1,0:T(8,128)S(1)}) fusion(f32[64,1024]{1,0:T(8,128)} %param.4, bf16[4,2048,1024]{2,1,0:T(8,128)(2,1)} %param.7, bf16[4,1024,2048]{2,1,0:T(8,128)(2,1)} %param.6, f32[1024]{0:T(1024)S(1)} %bitcast.351, f32[64]{0:T(128)S(1)} %add_rsqrt_fusion.20), kind=kOutput, calls=%fused_computation.443 | convolution fusion | flops 538443712 | bytes 9179648 | tf_op jit(solution)/shard_map/dot_general | solution.py:21
  8.0 5.4 %multiply_reduce_fusion.20 = (f32[64]{0:T(128)S(1)}, f32[64,1024]{1,0:T(8,128)S(1)}) fusion(f32[64,1024]{1,0:T(8,128)S(1)} %get-tuple-element.33, bf16[4,2048,1024]{2,1,0:T(8,128)(2,1)} %param.7, bf16[4,1024,2048]{2,1,0:T(8,128)(2,1)} %param.6, f32[1024]{0:T(1024)S(1)} %bitcast.338, f32[64]{0:T(128)S(1)} %add_rsqrt_fusion.19), kind=kOutput, calls=%fused_computation.441 | convolution fusion | flops 538443712 | bytes 9179904 | tf_op jit(solution)/shard_map/dot_general | solution.py:21
  13.4 5.3 %multiply_reduce_fusion.19 = (f32[64]{0:T(128)S(1)}, f32[64,1024]{1,0:T(8,128)S(1)}) fusion(f32[64,1024]{1,0:T(8,128)S(1)} %get-tuple-element.35, bf16[4,2048,1024]{2,1,0:T(8,128)(2,1)} %param.7, bf16[4,1024,2048]{2,1,0:T(8,128)(2,1)} %param.6, f32[1024]{0:T(1024)S(1)} %bitcast.334, f32[64]{0:T(128)S(1)} %add_rsqrt_fusion.18), kind=kOutput, calls=%fused_computation.439 | convolution fusion | flops 538443712 | bytes 9179904 | tf_op jit(solution)/shard_map/dot_general | solution.py:21
  18.8 5.2 %fusion.120 = f32[64,1024]{1,0:T(8,128)S(1)} fusion(f32[64,1024]{1,0:T(8,128)S(1)} %get-tuple-element.37, bf16[4,2048,1024]{2,1,0:T(8,128)(2,1)} %param.7, bf16[4,1024,2048]{2,1,0:T(8,128)(2,1)} %param.6, f32[1024]{0:T(1024)S(1)} %bitcast.342, f32[64]{0:T(128)S(1)} %add_rsqrt_fusion.17), kind=kOutput, calls=%fused_computation.121 | convolution fusion | flops 538312704 | bytes 9179648 | tf_op jit(solution)/shard_map/dot_general | solution.py:21
  24.0 4.9 %collective-permute-start.1 = (f32[64,1024]{1,0:T(8,128)S(1)}, f32[64,1024]{1,0:T(8,128)S(1)}, u32[]{:S(2)}, u32[]{:S(2)}) collective-permute-start(f32[64,1024]{1,0:T(8,128)S(1)} %fusion.120), channel_id=1, source_target_pairs={{0,16},{4,20},{8,24},{12,28},{1,17},{5,21},{9,25},{13,29},{2,18},{... | collective-permute-start | bytes 786440 | tf_op jit(solution)/shard_map/ppermute | solution.py:12
  28.9 1.7 collective-permute-start
  30.6 6.7 %collective-permute-done.1 = f32[64,1024]{1,0:T(8,128)S(1)} collective-permute-done((f32[64,1024]{1,0:T(8,128)S(1)}, f32[64,1024]{1,0:T(8,128)S(1)}, u32[]{:S(2)}, u32[]{:S(2)}) %collective-permute-start.1) | collective-permute-done | bytes 262176 | tf_op jit(solution)/shard_map/ppermute | solution.py:12
  37.4 5.3 %multiply_reduce_fusion.17 = (f32[64]{0:T(128)S(1)}, f32[64,1024]{1,0:T(8,128)S(1)}) fusion(f32[64,1024]{1,0:T(8,128)S(1)} %get-tuple-element.13, bf16[4,2048,1024]{2,1,0:T(8,128)(2,1)} %param.7, bf16[4,1024,2048]{2,1,0:T(8,128)(2,1)} %param.6, f32[64]{0:T(128)S(1)} %add_rsqrt_fusion.16, f32[1024]{0:T(1024)S(1)} %bitcast.352), kind=kOutput, calls=%fused_computation.435 | convolution fusion | flops 538443712 | bytes 9179904 | tf_op jit(solution)/shard_map/dot_general | solution.py:21
  42.7 5.3 %multiply_reduce_fusion.16 = (f32[64]{0:T(128)S(1)}, f32[64,1024]{1,0:T(8,128)S(1)}) fusion(f32[64,1024]{1,0:T(8,128)S(1)} %get-tuple-element.39, bf16[4,2048,1024]{2,1,0:T(8,128)(2,1)} %param.7, bf16[4,1024,2048]{2,1,0:T(8,128)(2,1)} %param.6, f32[64]{0:T(128)S(1)} %add_rsqrt_fusion.15, f32[1024]{0:T(1024)S(1)} %bitcast.339), kind=kOutput, calls=%fused_computation.433 | convolution fusion | flops 538443712 | bytes 9179904 | tf_op jit(solution)/shard_map/dot_general | solution.py:21
  48.1 5.2 %fusion.216 = f32[64,1024]{1,0:T(8,128)S(1)} fusion(f32[64,1024]{1,0:T(8,128)S(1)} %get-tuple-element.41, bf16[4,2048,1024]{2,1,0:T(8,128)(2,1)} %param.7, bf16[4,1024,2048]{2,1,0:T(8,128)(2,1)} %param.6, f32[64]{0:T(128)S(1)} %add_rsqrt_fusion.14, f32[1024]{0:T(1024)S(1)} %bitcast.335), kind=kOutput, calls=%fused_computation.153 | convolution fusion | flops 538312704 | bytes 9179648 | tf_op jit(solution)/shard_map/dot_general | solution.py:21
  53.5 5.7 %fusion.14 = f32[192,1024]{1,0:T(8,128)S(1)} fusion(f32[64,1024]{1,0:T(8,128)S(1)} %get-tuple-element.27, f32[64,1024]{1,0:T(8,128)S(1)} %get-tuple-element.13, f32[64,1024]{1,0:T(8,128)S(1)} %fusion.216, f32[1024]{0:T(1024)S(1)} %bitcast.343, f32[192]{0:T(256)S(1)} %add_rsqrt_fusion, bf16[4,2048,1024]{2,1,0:T(8,128)(2,1)} %param.7, ...), kind=kOutput, calls=%fused_computation.14 | convolution fusion | flops 1615134720 | bytes 9966336 | tf_op jit(solution)/shard_map/dot_general | solution.py:21
  59.9 1.3 collective-permute-start.2
  62.4 5.2 %fusion.192 = f32[64,1024]{1,0:T(8,128)S(1)} fusion(f32[64,1024]{1,0:T(8,128)S(1)} %get-tuple-element.14, f32[64,1024]{1,0:T(8,128)S(1)} %get-tuple-element.15, bf16[4,2048,1024]{2,1,0:T(8,128)(2,1)} %param.7, bf16[4,1024,2048]{2,1,0:T(8,128)(2,1)} %param.6, f32[64]{0:T(128)S(1)} %add_rsqrt_fusion.13, f32[1024]{0:T(1024)S(1)} %bitcast.344, pred[]{:T(512)S(6)} %eq.46, ...), kind=kOutput, calls=%fused_computation.145 | convolution fusion | flops 538640384 | bytes 10229760 | tf_op jit(solution)/shard_map/dot_general | solution.py:21
  67.7 5.6 %collective-permute-start.3 = (f32[64,1024]{1,0:T(8,128)S(1)}, f32[64,1024]{1,0:T(8,128)S(1)}, u32[]{:S(2)}, u32[]{:S(2)}) collective-permute-start(f32[64,1024]{1,0:T(8,128)S(1)} %fusion.192), channel_id=1, source_target_pairs={{0,4},{4,8},{8,12},{12,16},{16,20},{20,24},{24,28},{1,5},{5,9},{9,... | collective-permute-start | bytes 786440 | tf_op jit(solution)/shard_map/ppermute | solution.py:12
  74.6 5.2 %fusion.189 = f32[64,1024]{1,0:T(8,128)S(1)} fusion(f32[64,1024]{1,0:T(8,128)S(1)} %fusion.192, f32[64,1024]{1,0:T(8,128)S(1)} %get-tuple-element.15, bf16[4,2048,1024]{2,1,0:T(8,128)(2,1)} %param.7, bf16[4,1024,2048]{2,1,0:T(8,128)(2,1)} %param.6, f32[64]{0:T(128)S(1)} %add_rsqrt_fusion.12, f32[1024]{0:T(1024)S(1)} %bitcast.345, pred[]{:T(512)S(6)} %eq.23, ...), kind=kOutput, calls=%fused_computation.144 | convolution fusion | flops 538640384 | bytes 10229760 | tf_op jit(solution)/shard_map/dot_general | solution.py:21
  79.8 6.6 %collective-permute-start.4 = (f32[64,1024]{1,0:T(8,128)S(1)}, f32[64,1024]{1,0:T(8,128)S(1)}, u32[]{:S(2)}, u32[]{:S(2)}) collective-permute-start(f32[64,1024]{1,0:T(8,128)S(1)} %fusion.189), channel_id=1, source_target_pairs={{0,4},{4,8},{8,12},{12,16},{16,20},{20,24},{24,28},{1,5},{5,9},{9,... | collective-permute-start | bytes 786440 | tf_op jit(solution)/shard_map/ppermute | solution.py:12
  87.6 5.2 %fusion.186 = f32[64,1024]{1,0:T(8,128)S(1)} fusion(f32[64,1024]{1,0:T(8,128)S(1)} %fusion.189, f32[64,1024]{1,0:T(8,128)S(1)} %get-tuple-element.15, bf16[4,2048,1024]{2,1,0:T(8,128)(2,1)} %param.7, bf16[4,1024,2048]{2,1,0:T(8,128)(2,1)} %param.6, f32[64]{0:T(128)S(1)} %add_rsqrt_fusion.11, f32[1024]{0:T(1024)S(1)} %bitcast.346, pred[]{:T(512)S(6)} %eq.49, ...), kind=kOutput, calls=%fused_computation.143 | convolution fusion | flops 538640384 | bytes 10229760 | tf_op jit(solution)/shard_map/dot_general | solution.py:21
  92.9 6.6 %collective-permute-start.6 = (f32[64,1024]{1,0:T(8,128)S(1)}, f32[64,1024]{1,0:T(8,128)S(1)}, u32[]{:S(2)}, u32[]{:S(2)}) collective-permute-start(f32[64,1024]{1,0:T(8,128)S(1)} %fusion.186), channel_id=1, source_target_pairs={{0,4},{4,8},{8,12},{12,16},{16,20},{20,24},{24,28},{1,5},{5,9},{9,... | collective-permute-start | bytes 786440 | tf_op jit(solution)/shard_map/ppermute | solution.py:12
  99.4 8.8 %collective-permute-start.5 = (f32[64,1024]{1,0:T(8,128)S(1)}, f32[64,1024]{1,0:T(8,128)S(1)}, u32[]{:S(2)}, u32[]{:S(2)}) collective-permute-start(f32[64,1024]{1,0:T(8,128)S(1)} %fusion.186), channel_id=1, source_target_pairs={{0,16},{4,20},{8,24},{12,28},{1,17},{5,21},{9,25},{13,29},{2,18},{... | collective-permute-start | bytes 786440 | tf_op jit(solution)/shard_map/ppermute | solution.py:12
  108.3 4.8 %collective-permute-done.5 = f32[64,1024]{1,0:T(8,128)S(1)} collective-permute-done((f32[64,1024]{1,0:T(8,128)S(1)}, f32[64,1024]{1,0:T(8,128)S(1)}, u32[]{:S(2)}, u32[]{:S(2)}) %collective-permute-start.5) | collective-permute-done | bytes 262176 | tf_op jit(solution)/shard_map/ppermute | solution.py:12
  113.3 5.3 %fusion.183 = f32[64,1024]{1,0:T(8,128)S(1)} fusion(f32[64,1024]{1,0:T(8,128)S(1)} %fusion.186, f32[64,1024]{1,0:T(8,128)S(1)} %get-tuple-element.11, f32[64,1024]{1,0:T(8,128)S(1)} %get-tuple-element.15, f32[64,1024]{1,0:T(8,128)S(1)} %get-tuple-element.27, f32[192,1024]{1,0:T(8,128)S(1)} %fusion.14, bf16[4,2048,1024]{2,1,0:T(8,128)(2,1)} %param.7, ...), kind=kOutput, calls=%fused_computation.142 | convolution fusion | flops 538771456 | bytes 10228230 | tf_op jit(solution)/shard_map/dot_general | solution.py:21
  118.5 1.3 collective-permute-start.7
  119.8 1.1 collective-permute-done.7
  121.1 5.2 %fusion.180 = f32[64,1024]{1,0:T(8,128)S(1)} fusion(f32[64,1024]{1,0:T(8,128)S(1)} %fusion.183, f32[64,1024]{1,0:T(8,128)S(1)} %get-tuple-element.15, bf16[4,2048,1024]{2,1,0:T(8,128)(2,1)} %param.7, bf16[4,1024,2048]{2,1,0:T(8,128)(2,1)} %param.6, f32[64]{0:T(128)S(1)} %add_rsqrt_fusion.9, f32[1024]{0:T(1024)S(1)} %bitcast.348, pred[]{:T(512)S(6)} %eq.46, ...), kind=kOutput, calls=%fused_computation.141 | convolution fusion | flops 538640384 | bytes 10229760 | tf_op jit(solution)/shard_map/dot_general | solution.py:21
  126.3 2.3 collective-permute-start.8
  129.9 5.2 %fusion.177 = f32[64,1024]{1,0:T(8,128)S(1)} fusion(f32[64,1024]{1,0:T(8,128)S(1)} %fusion.180, f32[64,1024]{1,0:T(8,128)S(1)} %get-tuple-element.15, bf16[4,2048,1024]{2,1,0:T(8,128)(2,1)} %param.7, bf16[4,1024,2048]{2,1,0:T(8,128)(2,1)} %param.6, f32[64]{0:T(128)S(1)} %add_rsqrt_fusion.8, f32[1024]{0:T(1024)S(1)} %bitcast.349, pred[]{:T(512)S(6)} %eq.23, ...), kind=kOutput, calls=%fused_computation.140 | convolution fusion | flops 538640384 | bytes 10229760 | tf_op jit(solution)/shard_map/dot_general | solution.py:21
  135.1 15.7 %collective-permute-start.16 = (f32[64,1024]{1,0:T(8,128)S(1)}, f32[64,1024]{1,0:T(8,128)S(1)}, u32[]{:S(2)}, u32[]{:S(2)}) collective-permute-start(f32[64,1024]{1,0:T(8,128)S(1)} %fusion.177), channel_id=1, source_target_pairs={{0,16},{4,20},{8,24},{12,28},{1,17},{5,21},{9,25},{13,29},{2,18},{... | collective-permute-start | bytes 786440 | tf_op jit(solution)/shard_map/ppermute | solution.py:12
  150.9 1.3 collective-permute-start.9
  152.2 1.3 compare_select_fusion
  153.5 39.5 %all-reduce = (f32[7]{0:T(128)S(1)}, f32[7]{0:T(128)S(1)}) all-reduce(f32[7]{0:T(128)S(1)} %get-tuple-element.43, f32[7]{0:T(128)S(1)} %get-tuple-element.42), channel_id=1, replica_groups=mesh['layer'=8,'dp'=4] {'layer','dp'}, use_global_device_ids=true, to_apply=%region_18.19 | all-reduce | flops 14 | bytes 112 | tf_op jit(solution)/shard_map/psum | solution.py:262
  193.2 5.2 %fusion.201 = f32[64,1024]{1,0:T(8,128)S(1)} fusion(f32[64,1024]{1,0:T(8,128)S(1)} %get-tuple-element.9, bf16[4,2048,1024]{2,1,0:T(8,128)(2,1)} %param.7, bf16[4,1024,2048]{2,1,0:T(8,128)(2,1)} %param.6, f32[64]{0:T(128)S(1)} %add_rsqrt_fusion.7, f32[1024]{0:T(1024)S(1)} %bitcast.353), kind=kOutput, calls=%fused_computation.148 | convolution fusion | flops 538312704 | bytes 9179648 | tf_op jit(solution)/shard_map/dot_general | solution.py:21
  198.4 1.3 collective-permute-start.10
  200.3 4.8 %collective-permute-start.11 = (f32[64,1024]{1,0:T(8,128)S(1)}, f32[64,1024]{1,0:T(8,128)S(1)}, u32[]{:S(2)}, u32[]{:S(2)}) collective-permute-start(f32[64,1024]{1,0:T(8,128)S(1)} %fusion.201), channel_id=1, source_target_pairs={{0,16},{4,20},{8,24},{12,28},{1,17},{5,21},{9,25},{13,29},{2,18},{... | collective-permute-start | bytes 786440 | tf_op jit(solution)/shard_map/ppermute | solution.py:12
  205.2 7.2 %collective-permute-done.11 = f32[64,1024]{1,0:T(8,128)S(1)} collective-permute-done((f32[64,1024]{1,0:T(8,128)S(1)}, f32[64,1024]{1,0:T(8,128)S(1)}, u32[]{:S(2)}, u32[]{:S(2)}) %collective-permute-start.11) | collective-permute-done | bytes 262176 | tf_op jit(solution)/shard_map/ppermute | solution.py:12
  212.6 5.1 %fusion.68 = f32[128,1024]{1,0:T(8,128)S(1)} fusion(bf16[4,2048,1024]{2,1,0:T(8,128)(2,1)} %param.7, bf16[4,1024,2048]{2,1,0:T(8,128)(2,1)} %param.6, f32[128,1024]{1,0:T(8,128)S(1)} %constant_dynamic-update-slice_fusion, f32[1024]{0:T(1024)S(1)} %bitcast.354, f32[128]{0:T(128)S(1)} %add_rsqrt_fusion.4), kind=kOutput, calls=%fused_computation.68 | convolution fusion | flops 1076494336 | bytes 9441792 | tf_op jit(solution)/shard_map/dot_general | solution.py:21
  217.8 5.2 %fusion.210 = f32[64,1024]{1,0:T(8,128)S(1)} fusion(f32[64,1024]{1,0:T(8,128)S(1)} %fusion.201, bf16[4,2048,1024]{2,1,0:T(8,128)(2,1)} %param.7, bf16[4,1024,2048]{2,1,0:T(8,128)(2,1)} %param.6, f32[64]{0:T(128)S(1)} %add_rsqrt_fusion.6, f32[1024]{0:T(1024)S(1)} %bitcast.340), kind=kOutput, calls=%fused_computation.151 | convolution fusion | flops 538312704 | bytes 9179648 | tf_op jit(solution)/shard_map/dot_general | solution.py:21
  223.0 2.0 collective-permute-start.12
  225.0 4.7 %collective-permute-start.13 = (f32[64,1024]{1,0:T(8,128)S(1)}, f32[64,1024]{1,0:T(8,128)S(1)}, u32[]{:S(2)}, u32[]{:S(2)}) collective-permute-start(f32[64,1024]{1,0:T(8,128)S(1)} %fusion.210), channel_id=1, source_target_pairs={{0,16},{4,20},{8,24},{12,28},{1,17},{5,21},{9,25},{13,29},{2,18},{... | collective-permute-start | bytes 786440 | tf_op jit(solution)/shard_map/ppermute | solution.py:12
  229.7 5.8 %fusion = f32[128,1024]{1,0:T(8,128)} fusion(f32[64,1024]{1,0:T(8,128)S(1)} %get-tuple-element.26, f32[64,1024]{1,0:T(8,128)S(1)} %get-tuple-element.9, f32[1024]{0:T(1024)S(1)} %bitcast.350, f32[128]{0:T(128)S(1)} %add_rsqrt_fusion.1, bf16[4,2048,1024]{2,1,0:T(8,128)(2,1)} %param.7, bf16[4,1024,2048]{2,1,0:T(8,128)(2,1)} %param.6), kind=kOutput, calls=%fused_computation | convolution fusion | flops 1076625408 | bytes 9441792 | tf_op jit(solution)/shard_map/dot_general | solution.py:21
  235.5 1.7 collective-permute-done.13
  237.4 5.0 %fusion.52 = f32[128,1024]{1,0:T(8,128)S(1)} fusion(bf16[4,2048,1024]{2,1,0:T(8,128)(2,1)} %param.7, bf16[4,1024,2048]{2,1,0:T(8,128)(2,1)} %param.6, f32[128,1024]{1,0:T(8,128)S(1)} %constant_dynamic-update-slice_fusion.2, f32[1024]{0:T(1024)S(1)} %bitcast.341, f32[128]{0:T(128)S(1)} %add_rsqrt_fusion.3), kind=kOutput, calls=%fused_computation.52 | convolution fusion | flops 1076494336 | bytes 9441792 | tf_op jit(solution)/shard_map/dot_general | solution.py:21
  242.6 5.2 %fusion.219 = f32[64,1024]{1,0:T(8,128)S(1)} fusion(f32[64,1024]{1,0:T(8,128)S(1)} %fusion.210, bf16[4,2048,1024]{2,1,0:T(8,128)(2,1)} %param.7, bf16[4,1024,2048]{2,1,0:T(8,128)(2,1)} %param.6, f32[64]{0:T(128)S(1)} %add_rsqrt_fusion.5, f32[1024]{0:T(1024)S(1)} %bitcast.336), kind=kOutput, calls=%fused_computation.154 | convolution fusion | flops 538312704 | bytes 9179648 | tf_op jit(solution)/shard_map/dot_general | solution.py:21
  247.8 4.4 %collective-permute-start.15 = (f32[64,1024]{1,0:T(8,128)S(1)}, f32[64,1024]{1,0:T(8,128)S(1)}, u32[]{:S(2)}, u32[]{:S(2)}) collective-permute-start(f32[64,1024]{1,0:T(8,128)S(1)} %fusion.219), channel_id=1, source_target_pairs={{0,16},{4,20},{8,24},{12,28},{1,17},{5,21},{9,25},{13,29},{2,18},{... | collective-permute-start | bytes 786440 | tf_op jit(solution)/shard_map/ppermute | solution.py:12
  252.3 1.7 collective-permute-start.14
  255.0 2.0 pad_maximum_fusion
  257.1 3.7 %collective-permute-done.15 = f32[64,1024]{1,0:T(8,128)S(1)} collective-permute-done((f32[64,1024]{1,0:T(8,128)S(1)}, f32[64,1024]{1,0:T(8,128)S(1)}, u32[]{:S(2)}, u32[]{:S(2)}) %collective-permute-start.15) | collective-permute-done | bytes 262176 | tf_op jit(solution)/shard_map/ppermute | solution.py:12
  260.9 5.9 %fusion.36 = f32[128,1024]{1,0:T(8,128)} fusion(bf16[4,2048,1024]{2,1,0:T(8,128)(2,1)} %param.7, bf16[4,1024,2048]{2,1,0:T(8,128)(2,1)} %param.6, f32[128,1024]{1,0:T(8,128)S(1)} %constant_dynamic-update-slice_fusion.4, f32[1024]{0:T(1024)S(1)} %bitcast.337, f32[128]{0:T(128)S(1)} %add_rsqrt_fusion.2), kind=kOutput, calls=%fused_computation.36 | convolution fusion | flops 1076494336 | bytes 9441792 | tf_op jit(solution)/shard_map/dot_general | solution.py:21
  267.9 1.6 maximum_select_fusion
  (65 shorter events, 12.2 us)
Async XLA Ops:
  8.0 29.2 %copy-start = (f32[64,1024]{1,0:T(8,128)S(1)}, f32[64,1024]{1,0:T(8,128)}, u32[]{:S(2)}) copy-start(f32[64,1024]{1,0:T(8,128)} %param.4) | copy-start | bytes 786436
  24.0 13.3 %collective-permute-start.1 = (f32[64,1024]{1,0:T(8,128)S(1)}, f32[64,1024]{1,0:T(8,128)S(1)}, u32[]{:S(2)}, u32[]{:S(2)}) collective-permute-start(f32[64,1024]{1,0:T(8,128)S(1)} %fusion.120), channel_id=1, source_target_pairs={{0,16},{4,20},{8,24},{12,28},{1,17},{5,21},{9,25},{13,29},{2,18},{... | collective-permute-start | bytes 786440 | tf_op jit(solution)/shard_map/ppermute | solution.py:12
  28.9 8.3 %collective-permute-start = (f32[64,1024]{1,0:T(8,128)S(1)}, f32[64,1024]{1,0:T(8,128)S(1)}, u32[]{:S(2)}, u32[]{:S(2)}) collective-permute-start(f32[64,1024]{1,0:T(8,128)S(1)} %fusion.120), channel_id=1, source_target_pairs={{0,4},{4,8},{8,12},{12,16},{16,20},{20,24},{24,28},{1,5},{5,9},{9,... | collective-permute-start | bytes 786440 | tf_op jit(solution)/shard_map/ppermute | solution.py:12
  59.9 2.4 collective-permute-start.2
  67.7 6.8 %collective-permute-start.3 = (f32[64,1024]{1,0:T(8,128)S(1)}, f32[64,1024]{1,0:T(8,128)S(1)}, u32[]{:S(2)}, u32[]{:S(2)}) collective-permute-start(f32[64,1024]{1,0:T(8,128)S(1)} %fusion.192), channel_id=1, source_target_pairs={{0,4},{4,8},{8,12},{12,16},{16,20},{20,24},{24,28},{1,5},{5,9},{9,... | collective-permute-start | bytes 786440 | tf_op jit(solution)/shard_map/ppermute | solution.py:12
  79.8 7.7 %collective-permute-start.4 = (f32[64,1024]{1,0:T(8,128)S(1)}, f32[64,1024]{1,0:T(8,128)S(1)}, u32[]{:S(2)}, u32[]{:S(2)}) collective-permute-start(f32[64,1024]{1,0:T(8,128)S(1)} %fusion.189), channel_id=1, source_target_pairs={{0,4},{4,8},{8,12},{12,16},{16,20},{20,24},{24,28},{1,5},{5,9},{9,... | collective-permute-start | bytes 786440 | tf_op jit(solution)/shard_map/ppermute | solution.py:12
  92.9 15.4 %collective-permute-start.6 = (f32[64,1024]{1,0:T(8,128)S(1)}, f32[64,1024]{1,0:T(8,128)S(1)}, u32[]{:S(2)}, u32[]{:S(2)}) collective-permute-start(f32[64,1024]{1,0:T(8,128)S(1)} %fusion.186), channel_id=1, source_target_pairs={{0,4},{4,8},{8,12},{12,16},{16,20},{20,24},{24,28},{1,5},{5,9},{9,... | collective-permute-start | bytes 786440 | tf_op jit(solution)/shard_map/ppermute | solution.py:12
  99.4 13.7 %collective-permute-start.5 = (f32[64,1024]{1,0:T(8,128)S(1)}, f32[64,1024]{1,0:T(8,128)S(1)}, u32[]{:S(2)}, u32[]{:S(2)}) collective-permute-start(f32[64,1024]{1,0:T(8,128)S(1)} %fusion.186), channel_id=1, source_target_pairs={{0,16},{4,20},{8,24},{12,28},{1,17},{5,21},{9,25},{13,29},{2,18},{... | collective-permute-start | bytes 786440 | tf_op jit(solution)/shard_map/ppermute | solution.py:12
  118.5 2.4 collective-permute-start.7
  126.3 3.4 %collective-permute-start.8 = (f32[64,1024]{1,0:T(8,128)S(1)}, f32[64,1024]{1,0:T(8,128)S(1)}, u32[]{:S(2)}, u32[]{:S(2)}) collective-permute-start(f32[64,1024]{1,0:T(8,128)S(1)} %fusion.180), channel_id=1, source_target_pairs={{0,4},{4,8},{8,12},{12,16},{16,20},{20,24},{24,28},{1,5},{5,9},{9,... | collective-permute-start | bytes 786440 | tf_op jit(solution)/shard_map/ppermute | solution.py:12
  135.1 57.9 %collective-permute-start.16 = (f32[64,1024]{1,0:T(8,128)S(1)}, f32[64,1024]{1,0:T(8,128)S(1)}, u32[]{:S(2)}, u32[]{:S(2)}) collective-permute-start(f32[64,1024]{1,0:T(8,128)S(1)} %fusion.177), channel_id=1, source_target_pairs={{0,16},{4,20},{8,24},{12,28},{1,17},{5,21},{9,25},{13,29},{2,18},{... | collective-permute-start | bytes 786440 | tf_op jit(solution)/shard_map/ppermute | solution.py:12
  150.9 42.2 %collective-permute-start.9 = (f32[64,1024]{1,0:T(8,128)S(1)}, f32[64,1024]{1,0:T(8,128)S(1)}, u32[]{:S(2)}, u32[]{:S(2)}) collective-permute-start(f32[64,1024]{1,0:T(8,128)S(1)} %fusion.177), channel_id=1, source_target_pairs={{0,4},{4,8},{8,12},{12,16},{16,20},{20,24},{24,28},{1,5},{5,9},{9,... | collective-permute-start | bytes 786440 | tf_op jit(solution)/shard_map/ppermute | solution.py:12
  198.4 6.8 %collective-permute-start.10 = (f32[64,1024]{1,0:T(8,128)S(1)}, f32[64,1024]{1,0:T(8,128)S(1)}, u32[]{:S(2)}, u32[]{:S(2)}) collective-permute-start(f32[64,1024]{1,0:T(8,128)S(1)} %fusion.201), channel_id=1, source_target_pairs={{0,4},{4,8},{8,12},{12,16},{16,20},{20,24},{24,28},{1,5},{5,9},{9,... | collective-permute-start | bytes 786440 | tf_op jit(solution)/shard_map/ppermute | solution.py:12
  200.3 12.2 %collective-permute-start.11 = (f32[64,1024]{1,0:T(8,128)S(1)}, f32[64,1024]{1,0:T(8,128)S(1)}, u32[]{:S(2)}, u32[]{:S(2)}) collective-permute-start(f32[64,1024]{1,0:T(8,128)S(1)} %fusion.201), channel_id=1, source_target_pairs={{0,16},{4,20},{8,24},{12,28},{1,17},{5,21},{9,25},{13,29},{2,18},{... | collective-permute-start | bytes 786440 | tf_op jit(solution)/shard_map/ppermute | solution.py:12
  223.0 19.6 %copy-start.1 = (f32[64,1024]{1,0:T(8,128)}, f32[64,1024]{1,0:T(8,128)S(1)}, u32[]{:S(2)}) copy-start(f32[64,1024]{1,0:T(8,128)S(1)} %fusion.210) | copy-start | bytes 786436
  223.0 12.5 %collective-permute-start.12 = (f32[64,1024]{1,0:T(8,128)S(1)}, f32[64,1024]{1,0:T(8,128)S(1)}, u32[]{:S(2)}, u32[]{:S(2)}) collective-permute-start(f32[64,1024]{1,0:T(8,128)S(1)} %fusion.210), channel_id=1, source_target_pairs={{0,4},{4,8},{8,12},{12,16},{16,20},{20,24},{24,28},{1,5},{5,9},{9,... | collective-permute-start | bytes 786440 | tf_op jit(solution)/shard_map/ppermute | solution.py:12
  225.0 12.2 %collective-permute-start.13 = (f32[64,1024]{1,0:T(8,128)S(1)}, f32[64,1024]{1,0:T(8,128)S(1)}, u32[]{:S(2)}, u32[]{:S(2)}) collective-permute-start(f32[64,1024]{1,0:T(8,128)S(1)} %fusion.210), channel_id=1, source_target_pairs={{0,16},{4,20},{8,24},{12,28},{1,17},{5,21},{9,25},{13,29},{2,18},{... | collective-permute-start | bytes 786440 | tf_op jit(solution)/shard_map/ppermute | solution.py:12
  247.8 12.9 %collective-permute-start.15 = (f32[64,1024]{1,0:T(8,128)S(1)}, f32[64,1024]{1,0:T(8,128)S(1)}, u32[]{:S(2)}, u32[]{:S(2)}) collective-permute-start(f32[64,1024]{1,0:T(8,128)S(1)} %fusion.219), channel_id=1, source_target_pairs={{0,16},{4,20},{8,24},{12,28},{1,17},{5,21},{9,25},{13,29},{2,18},{... | collective-permute-start | bytes 786440 | tf_op jit(solution)/shard_map/ppermute | solution.py:12
  252.3 4.8 %collective-permute-start.14 = (f32[64,1024]{1,0:T(8,128)S(1)}, f32[64,1024]{1,0:T(8,128)S(1)}, u32[]{:S(2)}, u32[]{:S(2)}) collective-permute-start(f32[64,1024]{1,0:T(8,128)S(1)} %fusion.219), channel_id=1, source_target_pairs={{0,4},{4,8},{8,12},{12,16},{16,20},{20,24},{24,28},{1,5},{5,9},{9,... | collective-permute-start | bytes 786440 | tf_op jit(solution)/shard_map/ppermute | solution.py:12

commit v2 on v1

--- a/solution.py
+++ b/solution.py
@@ -1,6 +1,8 @@
 import jax
 import jax.numpy as jnp
 from jax import lax
+from jax.experimental import pallas as pl
+from jax.experimental.pallas import tpu as pltpu
 from jax.sharding import PartitionSpec as P
 
 epsilon = 1e-06
@@ -185,9 +187,210 @@
     return (layer_states, residual_ratios, defects_four, defects_sixteen)
 
 
+def coarse_kernel(
+    sections, copies,
+    initial, start, rhs_one, far_step, tile, gain, w_in, w_out,
+    point, left, far, totals,
+    cur, slots, ends, normed, total, across, along, summed,
+    send, arrive, end_arrive, across_send, across_arrive, along_send, along_arrive,
+):
+    here = lax.axis_index("layer")
+    depth = lax.axis_index("dp")
+    blocks = sections // 4
+    wide_end = blocks + 2
+    rounds = wide_end + 2
+    ff = w_in.shape[2]
+    width = ff // 4
+
+    def to(layer, dp):
+        return dict(device_id=(layer, dp), device_id_type=pl.DeviceIdType.MESH)
+
+    cur[...] = start[...]
+    across[depth] = tile[...]
+
+    barrier = pltpu.get_barrier_semaphore()
+    for k in range(1, sections):
+        pl.semaphore_signal(barrier, inc=1, **to(lax.rem(here + k, sections), depth))
+    for k in range(1, copies):
+        pl.semaphore_signal(barrier, inc=1, **to(here, lax.rem(depth + k, copies)))
+    pl.semaphore_wait(barrier, sections + copies - 2)
+
+    def across_copy(k):
+        return pltpu.make_async_remote_copy(
+            src_ref=tile, dst_ref=across.at[depth],
+            send_sem=across_send.at[k - 1], recv_sem=across_arrive.at[k - 1],
+            **to(here, lax.rem(depth + k, copies)),
+        )
+
+    for k in range(1, copies):
+        across_copy(k).start()
+
+    def wide(d, r):
+        return (r >= 3) & (r < wide_end) & (d == 4 * (r - 2) + 3)
+
+    def receives(d, r):
+        early = (r < 3) & (lax.rem(d, 4) == r + 1)
+        middle = (r >= 3) & (r < wide_end) & ((d == 4 * (r - 2)) | (d == 4 * (r - 2) + 3))
+        late = (r >= wide_end) & (lax.rem(d, 4) == r - wide_end + 1) & (d >= 4)
+        return early | middle | late
+
+    def hop(r, distance):
+        return pltpu.make_async_remote_copy(
+            src_ref=cur, dst_ref=slots.at[r], send_sem=send.at[distance // 4],
+            recv_sem=arrive.at[r], **to(lax.rem(here + distance, sections), depth),
+        )
+
+    def step(r, carry):
+        one = (here + 1 < sections) & receives(here + 1, r) & jnp.logical_not(wide(here + 1, r))
+        four = (here + 4 < sections) & wide(here + 4, r)
+
+        @pl.when(one)
+        def _():
+            hop(r, 1).start()
+
+        @pl.when(four)
+        def _():
+            hop(r, 4).start()
+
+        @pl.when(one)
+        def _():
+            hop(r, 1).wait_send()
+
+        @pl.when(four)
+        def _():
+            hop(r, 4).wait_send()
+
+        @pl.when(receives(here, r))
+        def _():
+            hop(r, 1).wait_recv()
+            before = slots[r]
+            mean_square = jnp.mean(before * before, axis=-1, keepdims=True)
+            normed[...] = (before * lax.rsqrt(mean_square + epsilon) * gain[...]).astype(
+                jnp.bfloat16
+            )
+            total[...] = jnp.zeros_like(total)
+
+            def part(i, c):
+                cols = pl.ds(pl.multiple_of(i * width, width), width)
+                hidden = jax.nn.gelu(
+                    jnp.dot(normed[...], w_in[0, :, cols], preferred_element_type=jnp.float32),
+                    approximate=True,
+                ).astype(jnp.bfloat16)
+                total[...] += jnp.dot(
+                    hidden, w_out[0, cols, :], preferred_element_type=jnp.float32
+                )
+                return c
+
+            lax.fori_loop(0, 4, part, 0)
+            is_wide = wide(here, r)
+
+            @pl.when(is_wide)
+            def _():
+                cur[...] = slots[r] + 16.0 * total[...] + (cur[...] - far_step[...])
+
+            @pl.when(jnp.logical_not(is_wide))
+            def _():
+                cur[...] = slots[r] + 4.0 * total[...] + rhs_one[...]
+
+        return carry
+
+    lax.fori_loop(0, rounds, step, 0)
+
+    def last(distance):
+        return pltpu.make_async_remote_copy(
+            src_ref=cur, dst_ref=ends.at[distance // 4], send_sem=send.at[distance // 4],
+            recv_sem=end_arrive.at[distance // 4],
+            **to(lax.rem(here + distance, sections), depth),
+        )
+
+    for distance in (1, 4):
+
+        @pl.when(here + distance < sections)
+        def _(distance=distance):
+            last(distance).start()
+
+    for k in range(1, copies):
+        across_copy(k).wait()
+    gathered = across[0]
+    for k in range(1, copies):
+        gathered = gathered + across[k]
+    summed[...] = gathered
+
+    def along_copy(k):
+        return pltpu.make_async_remote_copy(
+            src_ref=summed, dst_ref=along.at[k - 1],
+            send_sem=along_send.at[k - 1], recv_sem=along_arrive.at[k - 1],
+            **to(lax.rem(here + k, sections), depth),
+        )
+
+    for k in range(1, sections):
+        along_copy(k).start()
+    point[...] = cur[...]
+    for distance, out, edge in ((1, left, 1), (4, far, 4)):
+
+        @pl.when(here + distance < sections)
+        def _(distance=distance):
+            last(distance).wait_send()
+
+        @pl.when(here >= edge)
+        def _(distance=distance, out=out):
+            last(distance).wait_recv()
+            out[...] = ends[distance // 4]
+
+        @pl.when(here < edge)
+        def _(out=out):
+            out[...] = initial[...]
+
+    result = summed[...]
+    for k in range(1, sections):
+        along_copy(k).wait()
+        result = result + along[k - 1]
+    totals[...] = result
+
+
+def coarse(initial, start, rhs_one, far_step, tile, gain, first_weights, second_weights):
+    sections = lax.axis_size("layer")
+    copies = lax.axis_size("dp")
+    rounds = sections // 4 + 4
+    shape = initial.shape
+    d, ff = first_weights.shape[1:]
+    whole = pl.BlockSpec(shape, lambda i: (0, 0))
+    small = pl.BlockSpec((8, 128), lambda i: (0, 0))
+    state = jax.ShapeDtypeStruct(shape, jnp.float32)
+    dma = pltpu.SemaphoreType.DMA
+    return pl.pallas_call(
+        lambda *refs: coarse_kernel(sections, copies, *refs),
+        grid=(1,),
+        out_shape=(state, state, state, jax.ShapeDtypeStruct((8, 128), jnp.float32)),
+        in_specs=[
+            whole, whole, whole, whole, small,
+            pl.BlockSpec((1, d), lambda i: (0, 0)),
+            pl.BlockSpec((1, d, ff), lambda i: (3, 0, 0)),
+            pl.BlockSpec((1, ff, d), lambda i: (3, 0, 0)),
+        ],
+        out_specs=(whole, whole, whole, small),
+        scratch_shapes=[
+            pltpu.VMEM(shape, jnp.float32),
+            pltpu.VMEM((rounds,) + shape, jnp.float32),
+            pltpu.VMEM((2,) + shape, jnp.float32),
+            pltpu.VMEM(shape, jnp.bfloat16),
+            pltpu.VMEM(shape, jnp.float32),
+            pltpu.VMEM((copies, 8, 128), jnp.float32),
+            pltpu.VMEM((sections - 1, 8, 128), jnp.float32),
+            pltpu.VMEM((8, 128), jnp.float32),
+            dma((2,)), dma((rounds,)), dma((2,)),
+            dma((copies - 1,)), dma((copies - 1,)),
+            dma((sections - 1,)), dma((sections - 1,)),
+        ],
+        compiler_params=pltpu.CompilerParams(
+            collective_id=0, has_side_effects=True, vmem_limit_bytes=40 * 1024 * 1024
+        ),
+        name="coarse",
+    )(initial, start, rhs_one, far_step, tile, gain, first_weights, second_weights)
+
+
 def local_quads(initial, norm_gains, first_weights, second_weights):
     sections = lax.axis_size("layer")
-    blocks = sections // 4
     here = lax.axis_index("layer")
     place = here % 4
     rows = initial.shape[0]
@@ -221,26 +424,12 @@
     step_sum = jnp.sum(near_term * near_term)
 
     point = jnp.where(place == 0, fine, point)
-    for residue in (1, 2, 3):
-        before = near(point)
-        stepped = before + 4.0 * moved(3, before) + rhs_one
-        point = jnp.where(place == residue, stepped, point)
-    rhs_two = point - far_step
-
-    wide = place == 3
-    factor = jnp.where(wide, 16.0, 4.0)
-    source = jnp.where(wide, rhs_two, rhs_one)
-    for block in range(1, blocks):
-        before = jnp.where(wide, distant(point), near(point))
-        stepped = before + factor * moved(3, before) + source
-        point = jnp.where((here == 4 * block) | (here == 4 * block + 3), stepped, point)
-    for residue in (1, 2):
-        before = near(point)
-        stepped = before + 4.0 * moved(3, before) + rhs_one
-        point = jnp.where(place == residue, stepped, point)
-
-    left = near(point)
-    far = distant(point)
+    lane = jnp.arange(128)[None, :] == here - 1
+    row = jnp.arange(8)[:, None]
+    tile = jnp.where(lane & (row == 0), gap_sum, 0.0) + jnp.where(lane & (row == 1), step_sum, 0.0)
+    point, left, far, totals = coarse(
+        initial, point, rhs_one, far_step, tile, norm_gains[3:4], first_weights, second_weights
+    )
     state = left
     states = []
     for slot in range(3):
@@ -258,14 +447,14 @@
     points = here * 4 + jnp.arange(4, dtype=jnp.int32) + 1
     defects_four = jnp.where((points >= 4)[:, None, None], jnp.stack(fours), 0.0)
     defects_sixteen = jnp.where((points >= 16)[:, None, None], jnp.stack(sixteens), 0.0)
-    one_hot = (jnp.arange(sections - 1) == here - 1).astype(jnp.float32)
-    gap_total, step_total = lax.psum((gap_sum * one_hot, step_sum * one_hot), ("layer", "dp"))
+    gap_total = totals[0, : sections - 1]
+    step_total = totals[1, : sections - 1]
     ratios = jnp.sqrt(gap_total / (step_total + epsilon))
     return (jnp.stack(states), ratios, defects_four, defects_sixteen)
 
 
 def chosen(initial, norm_gains, first_weights, second_weights):
-    quads = first_weights.shape[0] == 4 and lax.axis_size("layer") % 4 == 0
+    quads = first_weights.shape[0] == 4 and lax.axis_size("layer") % 4 == 0 and lax.axis_size("dp") > 1
     return (local_quads if quads else local)(initial, norm_gains, first_weights, second_weights)
 
 

time: 270 us -> 190 us (0.70)
  starting transfers between devices: 74.9 us -> 24.5 us
  Pallas kernels: 0 us -> 45 us
  blocking collectives: 39.5 us -> 0 us
  matrix products: 112 us -> 79.7 us
    ppermute x17 -> x8, starting transfers between devices: 74.9 us -> 24.5 us  [shifted(): return lax.ppermute(block, axis, route)]
    pallas_call x0 -> x1, Pallas kernels: none -> 45 us  [coarse(): pl.pallas_call(lambda *refs: coarse_kernel(sections, copies, *refs), grid...]
    psum x1 -> x0, blocking collectives: 39.5 us -> none  [local_quads(): lax.psum((gap_sum * one_hot, step_sum * one_hot), ('layer', 'dp'))]
    dot_general x21 -> x15, matrix products: 112 us -> 79.7 us  [branch(): return jnp.dot(hidden, weight_out, preferred_element_type=jnp.float32)]
    ppermute x17 -> x8, waiting for transfers between devices: 29.7 us -> 29.2 us  [shifted(): return lax.ppermute(block, axis, route)]
  transfers between devices with their start and end apart: 17 -> 8, of which waited for: 10 -> 4; matrix products, arithmetic and copies ran while one was open for 4% -> 1% of each run, Pallas kernels for 0% -> 0%
where the time goes in v2:
time: 190 us
  matrix products  79.7 us (42%)
  Pallas kernels  45 us (24%)
  waiting for transfers between devices  29.2 us (15%)
  starting transfers between devices  24.5 us (13%)
  other arithmetic  9.61 us (5%)
    dot_general x15, matrix products, branch(): return jnp.dot(hidden, weight_out, preferred_element_type=jnp.float32)  79.7 us
    pallas_call x1, Pallas kernels, coarse(): pl.pallas_call(lambda *refs: coarse_kernel(sections, copies, *refs), grid...  45 us
    ppermute x8, waiting for transfers between devices, shifted(): return lax.ppermute(block, axis, route)  29.2 us
    ppermute x8, starting transfers between devices, shifted(): return lax.ppermute(block, axis, route)  24.5 us
  transfers between devices with their start and end apart: 8, of which 4 were waited for; matrix products, arithmetic and copies ran while one was open for 1% of the time, Pallas kernels for 0%

profile of v2, /device:TPU:0, one launch (start us, length us, event | category | flops | bytes accessed | tf_op | source)
XLA Modules:
  0.0 189.9 jit_solution(814263293313073322)
XLA Ops:
  0.6 0.9 fusion.537
  1.5 1.1 multiply_reduce_fusion.16
  2.6 5.4 %multiply_reduce_fusion.15 = (f32[64]{0:T(128)S(1)}, f32[64,1024]{1,0:T(8,128)S(1)}) fusion(f32[64,1024]{1,0:T(8,128)} %refs_0_.1, bf16[4,2048,1024]{2,1,0:T(8,128)(2,1)} %refs_7_.1, bf16[4,1024,2048]{2,1,0:T(8,128)(2,1)} %refs_6_.1, f32[1024]{0:T(1024)S(1)} %bitcast.239, f32[64]{0:T(128)S(1)} %add_rsqrt_fusion.14), kind=kOutput, calls=%fused_computation.331 | convolution fusion | flops 538443712 | bytes 9179648 | tf_op jit(solution)/shard_map/dot_general | solution.py:23
  8.0 0.0 copy-start
  8.0 5.4 %multiply_reduce_fusion.14 = (f32[64]{0:T(128)S(1)}, f32[64,1024]{1,0:T(8,128)S(1)}) fusion(f32[64,1024]{1,0:T(8,128)S(1)} %get-tuple-element.36, bf16[4,2048,1024]{2,1,0:T(8,128)(2,1)} %refs_7_.1, bf16[4,1024,2048]{2,1,0:T(8,128)(2,1)} %refs_6_.1, f32[1024]{0:T(1024)S(1)} %bitcast.235, f32[64]{0:T(128)S(1)} %add_rsqrt_fusion.13), kind=kOutput, calls=%fused_computation.329 | convolution fusion | flops 538443712 | bytes 9179904 | tf_op jit(solution)/shard_map/dot_general | solution.py:23
  13.4 5.3 %multiply_reduce_fusion.13 = (f32[64]{0:T(128)S(1)}, f32[64,1024]{1,0:T(8,128)S(1)}) fusion(f32[64,1024]{1,0:T(8,128)S(1)} %get-tuple-element.38, bf16[4,2048,1024]{2,1,0:T(8,128)(2,1)} %refs_7_.1, bf16[4,1024,2048]{2,1,0:T(8,128)(2,1)} %refs_6_.1, f32[1024]{0:T(1024)S(1)} %bitcast.231, f32[64]{0:T(128)S(1)} %add_rsqrt_fusion.12), kind=kOutput, calls=%fused_computation.327 | convolution fusion | flops 538443712 | bytes 9179904 | tf_op jit(solution)/shard_map/dot_general | solution.py:23
  18.8 5.2 %fusion.129 = f32[64,1024]{1,0:T(8,128)S(1)} fusion(f32[64,1024]{1,0:T(8,128)S(1)} %get-tuple-element.40, bf16[4,2048,1024]{2,1,0:T(8,128)(2,1)} %refs_7_.1, bf16[4,1024,2048]{2,1,0:T(8,128)(2,1)} %refs_6_.1, f32[1024]{0:T(1024)S(1)} %bitcast.225, f32[64]{0:T(128)S(1)} %add_rsqrt_fusion.11), kind=kOutput, calls=%fused_computation.112 | convolution fusion | flops 538312704 | bytes 9179648 | tf_op jit(solution)/shard_map/dot_general | solution.py:23
  24.0 2.4 %collective-permute-start = (f32[64,1024]{1,0:T(8,128)S(1)}, f32[64,1024]{1,0:T(8,128)S(1)}, u32[]{:S(2)}, u32[]{:S(2)}) collective-permute-start(f32[64,1024]{1,0:T(8,128)S(1)} %fusion.129), channel_id=1, source_target_pairs={{0,4},{4,8},{8,12},{12,16},{16,20},{20,24},{24,28},{1,5},{5,9},{9,... | collective-permute-start | bytes 786440 | tf_op jit(solution)/shard_map/ppermute | solution.py:14
  26.4 4.6 %collective-permute-start.1 = (f32[64,1024]{1,0:T(8,128)S(1)}, f32[64,1024]{1,0:T(8,128)S(1)}, u32[]{:S(2)}, u32[]{:S(2)}) collective-permute-start(f32[64,1024]{1,0:T(8,128)S(1)} %fusion.129), channel_id=1, source_target_pairs={{0,16},{4,20},{8,24},{12,28},{1,17},{5,21},{9,25},{13,29},{2,18},{... | collective-permute-start | bytes 786440 | tf_op jit(solution)/shard_map/ppermute | solution.py:14
  31.1 7.6 %collective-permute-done.1 = f32[64,1024]{1,0:T(8,128)S(1)} collective-permute-done((f32[64,1024]{1,0:T(8,128)S(1)}, f32[64,1024]{1,0:T(8,128)S(1)}, u32[]{:S(2)}, u32[]{:S(2)}) %collective-permute-start.1) | collective-permute-done | bytes 262176 | tf_op jit(solution)/shard_map/ppermute | solution.py:14
  38.7 0.1 multiply_reduce_fusion.12
  38.8 5.3 %multiply_reduce_fusion.11 = (f32[64]{0:T(128)S(1)}, f32[64,1024]{1,0:T(8,128)S(1)}) fusion(f32[64,1024]{1,0:T(8,128)S(1)} %get-tuple-element.15, bf16[4,2048,1024]{2,1,0:T(8,128)(2,1)} %refs_7_.1, bf16[4,1024,2048]{2,1,0:T(8,128)(2,1)} %refs_6_.1, f32[64]{0:T(128)S(1)} %add_rsqrt_fusion.10, f32[1024]{0:T(1024)S(1)} %bitcast.240), kind=kOutput, calls=%fused_computation.323 | convolution fusion | flops 538443712 | bytes 9179904 | tf_op jit(solution)/shard_map/dot_general | solution.py:23
  44.2 5.3 %multiply_reduce_fusion.10 = (f32[64]{0:T(128)S(1)}, f32[64,1024]{1,0:T(8,128)S(1)}) fusion(f32[64,1024]{1,0:T(8,128)S(1)} %get-tuple-element.42, bf16[4,2048,1024]{2,1,0:T(8,128)(2,1)} %refs_7_.1, bf16[4,1024,2048]{2,1,0:T(8,128)(2,1)} %refs_6_.1, f32[64]{0:T(128)S(1)} %add_rsqrt_fusion.9, f32[1024]{0:T(1024)S(1)} %bitcast.236), kind=kOutput, calls=%fused_computation.321 | convolution fusion | flops 538443712 | bytes 9179904 | tf_op jit(solution)/shard_map/dot_general | solution.py:23
  49.5 5.2 %fusion.123 = f32[64,1024]{1,0:T(8,128)S(1)} fusion(f32[64,1024]{1,0:T(8,128)S(1)} %get-tuple-element.44, bf16[4,2048,1024]{2,1,0:T(8,128)(2,1)} %refs_7_.1, bf16[4,1024,2048]{2,1,0:T(8,128)(2,1)} %refs_6_.1, f32[64]{0:T(128)S(1)} %add_rsqrt_fusion.8, f32[1024]{0:T(1024)S(1)} %bitcast.232), kind=kOutput, calls=%fused_computation.110 | convolution fusion | flops 538312704 | bytes 9179648 | tf_op jit(solution)/shard_map/dot_general | solution.py:23
  54.8 0.1 multiply_reduce_fusion
  54.9 5.7 %fusion.2 = f32[192,1024]{1,0:T(8,128)S(1)} fusion(bf16[4,2048,1024]{2,1,0:T(8,128)(2,1)} %refs_7_.1, bf16[4,1024,2048]{2,1,0:T(8,128)(2,1)} %refs_6_.1, f32[64,1024]{1,0:T(8,128)S(1)} %get-tuple-element.30, f32[64,1024]{1,0:T(8,128)S(1)} %get-tuple-element.15, f32[64,1024]{1,0:T(8,128)S(1)} %fusion.123, f32[1024]{0:T(1024)S(1)} %bitcast.226, ...), kind=kOutput, calls=%fused_computation.2 | convolution fusion | flops 1615134720 | bytes 9966336 | tf_op jit(solution)/shard_map/dot_general | solution.py:23
  60.6 0.7 multiply_reduce_fusion.9
  61.3 1.4 select_add_fusion.refs_4_
  62.7 45.0 %coarse.1 = (f32[64,1024]{1,0:T(8,128)S(1)}, f32[64,1024]{1,0:T(8,128)S(1)}, f32[64,1024]{1,0:T(8,128)S(1)}, f32[8,128]{1,0:T(8,128)S(1)}) custom-call(f32[64,1024]{1,0:T(8,128)S(1)} %copy-done, f32[64,1024]{1,0:T(8,128)S(1)} %get-tuple-element.16.refs_1_, f32[64,1024]{1,0:T(8,128)S(1)} %get-tuple-element.17.refs_2_, ...), custom_call_target="tpu_custom_call" | custom-call | tf_op jit(solution)/shard_map/coarse/pallas_call | solution.py:361
  107.8 0.1 multiply_reduce_fusion.1
  107.9 5.1 %fusion = f32[128,1024]{1,0:T(8,128)S(1)} fusion(bf16[4,2048,1024]{2,1,0:T(8,128)(2,1)} %refs_7_.1, bf16[4,1024,2048]{2,1,0:T(8,128)(2,1)} %refs_6_.1, f32[128,1024]{1,0:T(8,128)S(1)} %constant_dynamic-update-slice_fusion.6, f32[1024]{0:T(1024)S(1)} %bitcast.227, f32[128]{0:T(128)S(1)} %add_rsqrt_fusion.1), kind=kOutput, calls=%fused_computation | convolution fusion | flops 1076494336 | bytes 9441792 | tf_op jit(solution)/shard_map/dot_general | solution.py:23
  113.0 0.2 fusion.352
  113.1 5.2 %fusion.108 = f32[64,1024]{1,0:T(8,128)S(1)} fusion(f32[64,1024]{1,0:T(8,128)S(1)} %get-tuple-element.8, bf16[4,2048,1024]{2,1,0:T(8,128)(2,1)} %refs_7_.1, bf16[4,1024,2048]{2,1,0:T(8,128)(2,1)} %refs_6_.1, f32[64]{0:T(128)S(1)} %add_rsqrt_fusion.7, f32[1024]{0:T(1024)S(1)} %bitcast.241), kind=kOutput, calls=%fused_computation.105 | convolution fusion | flops 538312704 | bytes 9179648 | tf_op jit(solution)/shard_map/dot_general | solution.py:23
  118.4 2.0 %collective-permute-start.2 = (f32[64,1024]{1,0:T(8,128)S(1)}, f32[64,1024]{1,0:T(8,128)S(1)}, u32[]{:S(2)}, u32[]{:S(2)}) collective-permute-start(f32[64,1024]{1,0:T(8,128)S(1)} %fusion.108), channel_id=1, source_target_pairs={{0,4},{4,8},{8,12},{12,16},{16,20},{20,24},{24,28},{1,5},{5,9},{9,... | collective-permute-start | bytes 786440 | tf_op jit(solution)/shard_map/ppermute | solution.py:14
  120.4 2.8 %collective-permute-start.3 = (f32[64,1024]{1,0:T(8,128)S(1)}, f32[64,1024]{1,0:T(8,128)S(1)}, u32[]{:S(2)}, u32[]{:S(2)}) collective-permute-start(f32[64,1024]{1,0:T(8,128)S(1)} %fusion.108), channel_id=1, source_target_pairs={{0,16},{4,20},{8,24},{12,28},{1,17},{5,21},{9,25},{13,29},{2,18},{... | collective-permute-start | bytes 786440 | tf_op jit(solution)/shard_map/ppermute | solution.py:14
  123.2 0.0 collective-permute-done.2
  123.2 7.5 %collective-permute-done.3 = f32[64,1024]{1,0:T(8,128)S(1)} collective-permute-done((f32[64,1024]{1,0:T(8,128)S(1)}, f32[64,1024]{1,0:T(8,128)S(1)}, u32[]{:S(2)}, u32[]{:S(2)}) %collective-permute-start.3) | collective-permute-done | bytes 262176 | tf_op jit(solution)/shard_map/ppermute | solution.py:14
  130.7 0.1 multiply_reduce_fusion.4
  130.9 5.1 %fusion.44 = f32[128,1024]{1,0:T(8,128)S(1)} fusion(bf16[4,2048,1024]{2,1,0:T(8,128)(2,1)} %refs_7_.1, bf16[4,1024,2048]{2,1,0:T(8,128)(2,1)} %refs_6_.1, f32[128,1024]{1,0:T(8,128)S(1)} %constant_dynamic-update-slice_fusion, f32[1024]{0:T(1024)S(1)} %bitcast.242, f32[128]{0:T(128)S(1)} %add_rsqrt_fusion.4), kind=kOutput, calls=%fused_computation.44 | convolution fusion | flops 1076494336 | bytes 9441792 | tf_op jit(solution)/shard_map/dot_general | solution.py:23
  135.9 0.2 fusion.361
  136.1 5.2 %fusion.117 = f32[64,1024]{1,0:T(8,128)S(1)} fusion(f32[64,1024]{1,0:T(8,128)S(1)} %fusion.108, bf16[4,2048,1024]{2,1,0:T(8,128)(2,1)} %refs_7_.1, bf16[4,1024,2048]{2,1,0:T(8,128)(2,1)} %refs_6_.1, f32[64]{0:T(128)S(1)} %add_rsqrt_fusion.6, f32[1024]{0:T(1024)S(1)} %bitcast.237), kind=kOutput, calls=%fused_computation.108 | convolution fusion | flops 538312704 | bytes 9179648 | tf_op jit(solution)/shard_map/dot_general | solution.py:23
  141.4 1.9 %collective-permute-start.4 = (f32[64,1024]{1,0:T(8,128)S(1)}, f32[64,1024]{1,0:T(8,128)S(1)}, u32[]{:S(2)}, u32[]{:S(2)}) collective-permute-start(f32[64,1024]{1,0:T(8,128)S(1)} %fusion.117), channel_id=1, source_target_pairs={{0,4},{4,8},{8,12},{12,16},{16,20},{20,24},{24,28},{1,5},{5,9},{9,... | collective-permute-start | bytes 786440 | tf_op jit(solution)/shard_map/ppermute | solution.py:14
  143.3 4.4 %collective-permute-start.5 = (f32[64,1024]{1,0:T(8,128)S(1)}, f32[64,1024]{1,0:T(8,128)S(1)}, u32[]{:S(2)}, u32[]{:S(2)}) collective-permute-start(f32[64,1024]{1,0:T(8,128)S(1)} %fusion.117), channel_id=1, source_target_pairs={{0,16},{4,20},{8,24},{12,28},{1,17},{5,21},{9,25},{13,29},{2,18},{... | collective-permute-start | bytes 786440 | tf_op jit(solution)/shard_map/ppermute | solution.py:14
  147.8 7.8 %collective-permute-done.5 = f32[64,1024]{1,0:T(8,128)S(1)} collective-permute-done((f32[64,1024]{1,0:T(8,128)S(1)}, f32[64,1024]{1,0:T(8,128)S(1)}, u32[]{:S(2)}, u32[]{:S(2)}) %collective-permute-start.5) | collective-permute-done | bytes 262176 | tf_op jit(solution)/shard_map/ppermute | solution.py:14
  155.6 0.1 multiply_reduce_fusion.3
  155.7 5.9 %fusion.28 = f32[128,1024]{1,0:T(8,128)} fusion(bf16[4,2048,1024]{2,1,0:T(8,128)(2,1)} %refs_7_.1, bf16[4,1024,2048]{2,1,0:T(8,128)(2,1)} %refs_6_.1, f32[128,1024]{1,0:T(8,128)S(1)} %constant_dynamic-update-slice_fusion.2, f32[1024]{0:T(1024)S(1)} %bitcast.238, f32[128]{0:T(128)S(1)} %add_rsqrt_fusion.3), kind=kOutput, calls=%fused_computation.28 | convolution fusion | flops 1076494336 | bytes 9441792 | tf_op jit(solution)/shard_map/dot_general | solution.py:23
  161.6 1.2 fusion.358
  162.8 5.2 %fusion.126 = f32[64,1024]{1,0:T(8,128)S(1)} fusion(f32[64,1024]{1,0:T(8,128)S(1)} %fusion.117, bf16[4,2048,1024]{2,1,0:T(8,128)(2,1)} %refs_7_.1, bf16[4,1024,2048]{2,1,0:T(8,128)(2,1)} %refs_6_.1, f32[64]{0:T(128)S(1)} %add_rsqrt_fusion.5, f32[1024]{0:T(1024)S(1)} %bitcast.233), kind=kOutput, calls=%fused_computation.111 | convolution fusion | flops 538312704 | bytes 9179648 | tf_op jit(solution)/shard_map/dot_general | solution.py:23
  168.1 1.9 %collective-permute-start.6 = (f32[64,1024]{1,0:T(8,128)S(1)}, f32[64,1024]{1,0:T(8,128)S(1)}, u32[]{:S(2)}, u32[]{:S(2)}) collective-permute-start(f32[64,1024]{1,0:T(8,128)S(1)} %fusion.126), channel_id=1, source_target_pairs={{0,4},{4,8},{8,12},{12,16},{16,20},{20,24},{24,28},{1,5},{5,9},{9,... | collective-permute-start | bytes 786440 | tf_op jit(solution)/shard_map/ppermute | solution.py:14
  170.0 4.4 %collective-permute-start.7 = (f32[64,1024]{1,0:T(8,128)S(1)}, f32[64,1024]{1,0:T(8,128)S(1)}, u32[]{:S(2)}, u32[]{:S(2)}) collective-permute-start(f32[64,1024]{1,0:T(8,128)S(1)} %fusion.126), channel_id=1, source_target_pairs={{0,16},{4,20},{8,24},{12,28},{1,17},{5,21},{9,25},{13,29},{2,18},{... | collective-permute-start | bytes 786440 | tf_op jit(solution)/shard_map/ppermute | solution.py:14
  174.4 0.5 sqrt_bitcast_fusion
  174.9 1.1 pad_maximum_fusion
  176.0 6.3 %collective-permute-done.7 = f32[64,1024]{1,0:T(8,128)S(1)} collective-permute-done((f32[64,1024]{1,0:T(8,128)S(1)}, f32[64,1024]{1,0:T(8,128)S(1)}, u32[]{:S(2)}, u32[]{:S(2)}) %collective-permute-start.7) | collective-permute-done | bytes 262176 | tf_op jit(solution)/shard_map/ppermute | solution.py:14
  182.3 0.1 multiply_reduce_fusion.2
  182.4 5.0 %fusion.12 = f32[128,1024]{1,0:T(8,128)S(1)} fusion(bf16[4,2048,1024]{2,1,0:T(8,128)(2,1)} %refs_7_.1, bf16[4,1024,2048]{2,1,0:T(8,128)(2,1)} %refs_6_.1, f32[128,1024]{1,0:T(8,128)S(1)} %constant_dynamic-update-slice_fusion.4, f32[1024]{0:T(1024)S(1)} %bitcast.234, f32[128]{0:T(128)S(1)} %add_rsqrt_fusion.2), kind=kOutput, calls=%fused_computation.12 | convolution fusion | flops 1076494336 | bytes 9441792 | tf_op jit(solution)/shard_map/dot_general | solution.py:23
  187.5 0.1 fusion.355
  187.6 1.2 maximum_select_fusion.1
  188.7 1.2 maximum_select_fusion
  (30 shorter events, 0.3 us)
Async XLA Ops:
  8.0 30.6 %copy-start = (f32[64,1024]{1,0:T(8,128)S(1)}, f32[64,1024]{1,0:T(8,128)}, u32[]{:S(2)}) copy-start(f32[64,1024]{1,0:T(8,128)} %refs_0_.1) | copy-start | bytes 786436
  24.0 7.1 %collective-permute-start = (f32[64,1024]{1,0:T(8,128)S(1)}, f32[64,1024]{1,0:T(8,128)S(1)}, u32[]{:S(2)}, u32[]{:S(2)}) collective-permute-start(f32[64,1024]{1,0:T(8,128)S(1)} %fusion.129), channel_id=1, source_target_pairs={{0,4},{4,8},{8,12},{12,16},{16,20},{20,24},{24,28},{1,5},{5,9},{9,... | collective-permute-start | bytes 786440 | tf_op jit(solution)/shard_map/ppermute | solution.py:14
  26.4 12.2 %collective-permute-start.1 = (f32[64,1024]{1,0:T(8,128)S(1)}, f32[64,1024]{1,0:T(8,128)S(1)}, u32[]{:S(2)}, u32[]{:S(2)}) collective-permute-start(f32[64,1024]{1,0:T(8,128)S(1)} %fusion.129), channel_id=1, source_target_pairs={{0,16},{4,20},{8,24},{12,28},{1,17},{5,21},{9,25},{13,29},{2,18},{... | collective-permute-start | bytes 786440 | tf_op jit(solution)/shard_map/ppermute | solution.py:14
  118.4 4.8 %collective-permute-start.2 = (f32[64,1024]{1,0:T(8,128)S(1)}, f32[64,1024]{1,0:T(8,128)S(1)}, u32[]{:S(2)}, u32[]{:S(2)}) collective-permute-start(f32[64,1024]{1,0:T(8,128)S(1)} %fusion.108), channel_id=1, source_target_pairs={{0,4},{4,8},{8,12},{12,16},{16,20},{20,24},{24,28},{1,5},{5,9},{9,... | collective-permute-start | bytes 786440 | tf_op jit(solution)/shard_map/ppermute | solution.py:14
  120.4 10.3 %collective-permute-start.3 = (f32[64,1024]{1,0:T(8,128)S(1)}, f32[64,1024]{1,0:T(8,128)S(1)}, u32[]{:S(2)}, u32[]{:S(2)}) collective-permute-start(f32[64,1024]{1,0:T(8,128)S(1)} %fusion.108), channel_id=1, source_target_pairs={{0,16},{4,20},{8,24},{12,28},{1,17},{5,21},{9,25},{13,29},{2,18},{... | collective-permute-start | bytes 786440 | tf_op jit(solution)/shard_map/ppermute | solution.py:14
  141.4 6.4 %collective-permute-start.4 = (f32[64,1024]{1,0:T(8,128)S(1)}, f32[64,1024]{1,0:T(8,128)S(1)}, u32[]{:S(2)}, u32[]{:S(2)}) collective-permute-start(f32[64,1024]{1,0:T(8,128)S(1)} %fusion.117), channel_id=1, source_target_pairs={{0,4},{4,8},{8,12},{12,16},{16,20},{20,24},{24,28},{1,5},{5,9},{9,... | collective-permute-start | bytes 786440 | tf_op jit(solution)/shard_map/ppermute | solution.py:14
  143.3 12.3 %collective-permute-start.5 = (f32[64,1024]{1,0:T(8,128)S(1)}, f32[64,1024]{1,0:T(8,128)S(1)}, u32[]{:S(2)}, u32[]{:S(2)}) collective-permute-start(f32[64,1024]{1,0:T(8,128)S(1)} %fusion.117), channel_id=1, source_target_pairs={{0,16},{4,20},{8,24},{12,28},{1,17},{5,21},{9,25},{13,29},{2,18},{... | collective-permute-start | bytes 786440 | tf_op jit(solution)/shard_map/ppermute | solution.py:14
  168.1 7.9 %collective-permute-start.6 = (f32[64,1024]{1,0:T(8,128)S(1)}, f32[64,1024]{1,0:T(8,128)S(1)}, u32[]{:S(2)}, u32[]{:S(2)}) collective-permute-start(f32[64,1024]{1,0:T(8,128)S(1)} %fusion.126), channel_id=1, source_target_pairs={{0,4},{4,8},{8,12},{12,16},{16,20},{20,24},{24,28},{1,5},{5,9},{9,... | collective-permute-start | bytes 786440 | tf_op jit(solution)/shard_map/ppermute | solution.py:14
  170.0 12.3 %collective-permute-start.7 = (f32[64,1024]{1,0:T(8,128)S(1)}, f32[64,1024]{1,0:T(8,128)S(1)}, u32[]{:S(2)}, u32[]{:S(2)}) collective-permute-start(f32[64,1024]{1,0:T(8,128)S(1)} %fusion.126), channel_id=1, source_target_pairs={{0,16},{4,20},{8,24},{12,28},{1,17},{5,21},{9,25},{13,29},{2,18},{... | collective-permute-start | bytes 786440 | tf_op jit(solution)/shard_map/ppermute | solution.py:14

commit v3 on v2

--- a/solution.py
+++ b/solution.py
@@ -436,8 +436,9 @@
         state = state + moved(slot, state)
         states.append(state)
     states.append(point)
-    lefts = [shifted(s, "layer", 1) for s in states[:3]] + [left]
-    fars = [shifted(s, "layer", 4) for s in states[:3]] + [far]
+    inner = jnp.stack(states[:3])
+    lefts = list(shifted(inner, "layer", 1)) + [left]
+    fars = list(shifted(inner, "layer", 4)) + [far]
     fours = []
     sixteens = []
     for slot in range(4):

time: 190 us -> 185 us (0.974)
  starting transfers between devices: 24.5 us -> 11.6 us
  other arithmetic: 9.61 us -> 11.8 us
  matrix products: 79.7 us -> 81.8 us
  local copies, waits for them, and re-layouts: 1.04 us -> 3.06 us
    ppermute x8 -> x4, starting transfers between devices: 24.5 us -> 11.6 us  [shifted(): return lax.ppermute(block, axis, route)]
    dot_general x15, matrix products: 79.7 us -> 81.8 us  [branch(): return jnp.dot(hidden, weight_out, preferred_element_type=jnp.float32)]
    ppermute x8 -> x4, waiting for transfers between devices: 29.2 us -> 30.1 us  [shifted(): return lax.ppermute(block, axis, route)]
  transfers between devices with their start and end apart: 8 -> 4, of which waited for: 4 -> 2; matrix products, arithmetic and copies ran while one was open for 1% -> 1% of each run, Pallas kernels for 0% -> 0%
where the time goes in v3:
time: 185 us; the launch traced here: 184 us
  matrix products  81.8 us (44%)
  Pallas kernels  45.2 us (24%)
  waiting for transfers between devices  30.1 us (16%)
  other arithmetic  11.8 us (6%)
  starting transfers between devices  11.6 us (6%)
  local copies, waits for them, and re-layouts  3.06 us (2%)
    dot_general x15, matrix products, branch(): return jnp.dot(hidden, weight_out, preferred_element_type=jnp.float32)  81.8 us
    pallas_call x1, Pallas kernels, coarse(): pl.pallas_call(lambda *refs: coarse_kernel(sections, copies, *refs), grid...  45.2 us
    ppermute x4, waiting for transfers between devices, shifted(): return lax.ppermute(block, axis, route)  30.1 us
    ppermute x4, starting transfers between devices, shifted(): return lax.ppermute(block, axis, route)  11.6 us
  transfers between devices with their start and end apart: 4, of which 2 were waited for; matrix products, arithmetic and copies ran while one was open for 1% of the time, Pallas kernels for 0%

profile of v3, /device:TPU:0, one launch (start us, length us, event | category | flops | bytes accessed | tf_op | source)
XLA Modules:
  0.0 184.4 jit_solution(10556816134786441955)
XLA Ops:
  0.6 0.9 fusion.543
  1.5 1.1 multiply_reduce_fusion.16
  2.6 5.4 %multiply_reduce_fusion.15 = (f32[64]{0:T(128)S(1)}, f32[64,1024]{1,0:T(8,128)S(1)}) fusion(f32[64,1024]{1,0:T(8,128)} %refs_0_.1, bf16[4,2048,1024]{2,1,0:T(8,128)(2,1)} %refs_7_.1, bf16[4,1024,2048]{2,1,0:T(8,128)(2,1)} %refs_6_.1, f32[1024]{0:T(1024)S(1)} %bitcast.266, f32[64]{0:T(128)S(1)} %add_rsqrt_fusion.14), kind=kOutput, calls=%fused_computation.341 | convolution fusion | flops 538443712 | bytes 9179648 | tf_op jit(solution)/shard_map/dot_general | solution.py:23
  8.0 0.0 copy-start
  8.0 5.4 %multiply_reduce_fusion.14 = (f32[64]{0:T(128)S(1)}, f32[64,1024]{1,0:T(8,128)S(1)}) fusion(f32[64,1024]{1,0:T(8,128)S(1)} %get-tuple-element.40, bf16[4,2048,1024]{2,1,0:T(8,128)(2,1)} %refs_7_.1, bf16[4,1024,2048]{2,1,0:T(8,128)(2,1)} %refs_6_.1, f32[1024]{0:T(1024)S(1)} %bitcast.274, f32[64]{0:T(128)S(1)} %add_rsqrt_fusion.13), kind=kOutput, calls=%fused_computation.339 | convolution fusion | flops 538443712 | bytes 9179904 | tf_op jit(solution)/shard_map/dot_general | solution.py:23
  13.4 5.3 %multiply_reduce_fusion.13 = (f32[64]{0:T(128)S(1)}, f32[64,1024]{1,0:T(8,128)S(1)}) fusion(f32[64,1024]{1,0:T(8,128)S(1)} %get-tuple-element.42, bf16[4,2048,1024]{2,1,0:T(8,128)(2,1)} %refs_7_.1, bf16[4,1024,2048]{2,1,0:T(8,128)(2,1)} %refs_6_.1, f32[1024]{0:T(1024)S(1)} %bitcast.270, f32[64]{0:T(128)S(1)} %add_rsqrt_fusion.12), kind=kOutput, calls=%fused_computation.337 | convolution fusion | flops 538443712 | bytes 9179904 | tf_op jit(solution)/shard_map/dot_general | solution.py:23
  18.8 5.2 %fusion.129 = f32[64,1024]{1,0:T(8,128)S(1)} fusion(f32[64,1024]{1,0:T(8,128)S(1)} %get-tuple-element.44, bf16[4,2048,1024]{2,1,0:T(8,128)(2,1)} %refs_7_.1, bf16[4,1024,2048]{2,1,0:T(8,128)(2,1)} %refs_6_.1, f32[1024]{0:T(1024)S(1)} %bitcast.257, f32[64]{0:T(128)S(1)} %add_rsqrt_fusion.11), kind=kOutput, calls=%fused_computation.112 | convolution fusion | flops 538312704 | bytes 9179648 | tf_op jit(solution)/shard_map/dot_general | solution.py:23
  24.0 2.4 %collective-permute-start = (f32[64,1024]{1,0:T(8,128)S(1)}, f32[64,1024]{1,0:T(8,128)S(1)}, u32[]{:S(2)}, u32[]{:S(2)}) collective-permute-start(f32[64,1024]{1,0:T(8,128)S(1)} %fusion.129), channel_id=1, source_target_pairs={{0,4},{4,8},{8,12},{12,16},{16,20},{20,24},{24,28},{1,5},{5,9},{9,... | collective-permute-start | bytes 786440 | tf_op jit(solution)/shard_map/ppermute | solution.py:14
  26.4 4.6 %collective-permute-start.1 = (f32[64,1024]{1,0:T(8,128)S(1)}, f32[64,1024]{1,0:T(8,128)S(1)}, u32[]{:S(2)}, u32[]{:S(2)}) collective-permute-start(f32[64,1024]{1,0:T(8,128)S(1)} %fusion.129), channel_id=1, source_target_pairs={{0,16},{4,20},{8,24},{12,28},{1,17},{5,21},{9,25},{13,29},{2,18},{... | collective-permute-start | bytes 786440 | tf_op jit(solution)/shard_map/ppermute | solution.py:14
  31.1 0.0 collective-permute-done
  31.1 7.6 %collective-permute-done.1 = f32[64,1024]{1,0:T(8,128)S(1)} collective-permute-done((f32[64,1024]{1,0:T(8,128)S(1)}, f32[64,1024]{1,0:T(8,128)S(1)}, u32[]{:S(2)}, u32[]{:S(2)}) %collective-permute-start.1) | collective-permute-done | bytes 262176 | tf_op jit(solution)/shard_map/ppermute | solution.py:14
  38.7 0.0 copy-done
  38.7 0.1 multiply_reduce_fusion.12
  38.8 5.3 %multiply_reduce_fusion.11 = (f32[64]{0:T(128)S(1)}, f32[64,1024]{1,0:T(8,128)S(1)}) fusion(f32[64,1024]{1,0:T(8,128)S(1)} %get-tuple-element.15, bf16[4,2048,1024]{2,1,0:T(8,128)(2,1)} %refs_7_.1, bf16[4,1024,2048]{2,1,0:T(8,128)(2,1)} %refs_6_.1, f32[64]{0:T(128)S(1)} %add_rsqrt_fusion.10, f32[1024]{0:T(1024)S(1)} %bitcast.267), kind=kOutput, calls=%fused_computation.333 | convolution fusion | flops 538443712 | bytes 9179904 | tf_op jit(solution)/shard_map/dot_general | solution.py:23
  44.2 5.3 %multiply_reduce_fusion.10 = (f32[64]{0:T(128)S(1)}, f32[64,1024]{1,0:T(8,128)S(1)}) fusion(f32[64,1024]{1,0:T(8,128)S(1)} %get-tuple-element.46, bf16[4,2048,1024]{2,1,0:T(8,128)(2,1)} %refs_7_.1, bf16[4,1024,2048]{2,1,0:T(8,128)(2,1)} %refs_6_.1, f32[64]{0:T(128)S(1)} %add_rsqrt_fusion.9, f32[1024]{0:T(1024)S(1)} %bitcast.275), kind=kOutput, calls=%fused_computation.331 | convolution fusion | flops 538443712 | bytes 9179904 | tf_op jit(solution)/shard_map/dot_general | solution.py:23
  49.5 5.2 %fusion.123 = f32[64,1024]{1,0:T(8,128)S(1)} fusion(f32[64,1024]{1,0:T(8,128)S(1)} %get-tuple-element.48, bf16[4,2048,1024]{2,1,0:T(8,128)(2,1)} %refs_7_.1, bf16[4,1024,2048]{2,1,0:T(8,128)(2,1)} %refs_6_.1, f32[64]{0:T(128)S(1)} %add_rsqrt_fusion.8, f32[1024]{0:T(1024)S(1)} %bitcast.271), kind=kOutput, calls=%fused_computation.110 | convolution fusion | flops 538312704 | bytes 9179648 | tf_op jit(solution)/shard_map/dot_general | solution.py:23
  54.8 0.1 multiply_reduce_fusion
  54.9 5.7 %fusion.2 = f32[192,1024]{1,0:T(8,128)S(1)} fusion(bf16[4,2048,1024]{2,1,0:T(8,128)(2,1)} %refs_7_.1, bf16[4,1024,2048]{2,1,0:T(8,128)(2,1)} %refs_6_.1, f32[64,1024]{1,0:T(8,128)S(1)} %get-tuple-element.34, f32[64,1024]{1,0:T(8,128)S(1)} %get-tuple-element.15, f32[64,1024]{1,0:T(8,128)S(1)} %fusion.123, f32[1024]{0:T(1024)S(1)} %bitcast.258, ...), kind=kOutput, calls=%fused_computation.2 | convolution fusion | flops 1615134720 | bytes 9966336 | tf_op jit(solution)/shard_map/dot_general | solution.py:23
  60.6 0.7 multiply_reduce_fusion.9
  61.4 1.4 select_add_fusion.refs_4_
  62.7 45.2 %coarse.1 = (f32[64,1024]{1,0:T(8,128)S(1)}, f32[64,1024]{1,0:T(8,128)S(1)}, f32[64,1024]{1,0:T(8,128)S(1)}, f32[8,128]{1,0:T(8,128)S(1)}) custom-call(f32[64,1024]{1,0:T(8,128)S(1)} %copy-done, f32[64,1024]{1,0:T(8,128)S(1)} %get-tuple-element.16.refs_1_, f32[64,1024]{1,0:T(8,128)S(1)} %get-tuple-element.17.refs_2_, ...), custom_call_target="tpu_custom_call" | custom-call | tf_op jit(solution)/shard_map/coarse/pallas_call | solution.py:361
  108.0 0.1 multiply_reduce_fusion.1
  108.1 5.1 %fusion = f32[128,1024]{1,0:T(8,128)S(1)} fusion(bf16[4,2048,1024]{2,1,0:T(8,128)(2,1)} %refs_7_.1, bf16[4,1024,2048]{2,1,0:T(8,128)(2,1)} %refs_6_.1, f32[128,1024]{1,0:T(8,128)S(1)} %constant_dynamic-update-slice_fusion, f32[1024]{0:T(1024)S(1)} %bitcast.259, f32[128]{0:T(128)S(1)} %add_rsqrt_fusion.1), kind=kOutput, calls=%fused_computation | convolution fusion | flops 1076494336 | bytes 9441792 | tf_op jit(solution)/shard_map/dot_general | solution.py:23
  113.2 0.2 fusion.352
  113.4 5.3 %multiply_reduce_fusion.6 = (f32[64]{0:T(128)S(1)}, f32[64,1024]{1,0:T(8,128)S(1)}) fusion(f32[64,1024]{1,0:T(8,128)S(1)} %get-tuple-element.8, bf16[4,2048,1024]{2,1,0:T(8,128)(2,1)} %refs_7_.1, bf16[4,1024,2048]{2,1,0:T(8,128)(2,1)} %refs_6_.1, f32[64]{0:T(128)S(1)} %add_rsqrt_fusion.7, f32[1024]{0:T(1024)S(1)} %bitcast.268), kind=kOutput, calls=%fused_computation.325 | convolution fusion | flops 538443712 | bytes 9179904 | tf_op jit(solution)/shard_map/dot_general | solution.py:23
  118.7 5.3 %multiply_reduce_fusion.5 = (f32[64]{0:T(128)S(1)}, f32[64,1024]{1,0:T(8,128)S(1)}) fusion(f32[64,1024]{1,0:T(8,128)S(1)} %get-tuple-element.50, bf16[4,2048,1024]{2,1,0:T(8,128)(2,1)} %refs_7_.1, bf16[4,1024,2048]{2,1,0:T(8,128)(2,1)} %refs_6_.1, f32[64]{0:T(128)S(1)} %add_rsqrt_fusion.6, f32[1024]{0:T(1024)S(1)} %bitcast.276), kind=kOutput, calls=%fused_computation.323 | convolution fusion | flops 538443712 | bytes 9179904 | tf_op jit(solution)/shard_map/dot_general | solution.py:23
  124.1 5.2 %fusion.126 = f32[64,1024]{1,0:T(8,128)S(1)} fusion(f32[64,1024]{1,0:T(8,128)S(1)} %get-tuple-element.52, bf16[4,2048,1024]{2,1,0:T(8,128)(2,1)} %refs_7_.1, bf16[4,1024,2048]{2,1,0:T(8,128)(2,1)} %refs_6_.1, f32[64]{0:T(128)S(1)} %add_rsqrt_fusion.5, f32[1024]{0:T(1024)S(1)} %bitcast.272), kind=kOutput, calls=%fused_computation.111 | convolution fusion | flops 538312704 | bytes 9179648 | tf_op jit(solution)/shard_map/dot_general | solution.py:23
  129.3 0.9 pad_maximum_fusion.2
  130.2 2.1 %collective-permute-start.2 = (f32[3,64,1024]{2,1,0:T(8,128)}, f32[3,64,1024]{2,1,0:T(8,128)S(1)}, u32[]{:S(2)}, u32[]{:S(2)}) collective-permute-start(f32[3,64,1024]{2,1,0:T(8,128)} %pad_maximum_fusion.2), channel_id=1, source_target_pairs={{0,4},{4,8},{8,12},{12,16},{16,20},{20,24},{24,28},{1,5},{5,9},{9,... | collective-permute-start | bytes 2359304 | tf_op jit(solution)/shard_map/ppermute | solution.py:14
  132.3 2.5 %collective-permute-start.3 = (f32[3,64,1024]{2,1,0:T(8,128)}, f32[3,64,1024]{2,1,0:T(8,128)S(1)}, u32[]{:S(2)}, u32[]{:S(2)}) collective-permute-start(f32[3,64,1024]{2,1,0:T(8,128)} %pad_maximum_fusion.2), channel_id=1, source_target_pairs={{0,16},{4,20},{8,24},{12,28},{1,17},{5,21},{9,25},{13,29},{2,18},{... | collective-permute-start | bytes 2359304 | tf_op jit(solution)/shard_map/ppermute | solution.py:14
  134.9 1.1 pad_maximum_fusion
  135.9 0.5 sqrt_bitcast_fusion
  136.4 0.0 collective-permute-done.2
  136.4 0.8 slice_bitcast_fusion.5
  137.2 0.0 copy-start.1
  137.2 22.5 %collective-permute-done.3 = f32[3,64,1024]{2,1,0:T(8,128)S(1)} collective-permute-done((f32[3,64,1024]{2,1,0:T(8,128)}, f32[3,64,1024]{2,1,0:T(8,128)S(1)}, u32[]{:S(2)}, u32[]{:S(2)}) %collective-permute-start.3) | collective-permute-done | bytes 786464 | tf_op jit(solution)/shard_map/ppermute | solution.py:14
  159.8 0.8 slice_bitcast_fusion.4
  160.5 0.0 copy-done.1
  160.5 0.1 multiply_reduce_fusion.3
  160.6 0.6 copy-done.2
  161.2 6.0 %fusion.28 = f32[128,1024]{1,0:T(8,128)} fusion(bf16[4,2048,1024]{2,1,0:T(8,128)(2,1)} %refs_7_.1, bf16[4,1024,2048]{2,1,0:T(8,128)(2,1)} %refs_6_.1, f32[64,1024]{1,0:T(8,128)} %copy-done.2, f32[64,1024]{1,0:T(8,128)} %copy-done.1, f32[1024]{0:T(1024)S(1)} %bitcast.277, f32[128]{0:T(128)S(1)} %add_rsqrt_fusion.3), kind=kOutput, calls=%fused_computation.28 | convolution fusion | flops 1076625408 | bytes 9441792 | tf_op jit(solution)/shard_map/dot_general | solution.py:23
  167.3 1.1 multiply_reduce_fusion.2
  168.4 6.0 %fusion.12 = f32[128,1024]{1,0:T(8,128)} fusion(bf16[4,2048,1024]{2,1,0:T(8,128)(2,1)} %refs_7_.1, bf16[4,1024,2048]{2,1,0:T(8,128)(2,1)} %refs_6_.1, f32[64,1024]{1,0:T(8,128)} %get-tuple-element.30, f32[64,1024]{1,0:T(8,128)} %get-tuple-element.27, f32[1024]{0:T(1024)S(1)} %bitcast.273, f32[128]{0:T(128)S(1)} %add_rsqrt_fusion.2), kind=kOutput, calls=%fused_computation.12 | convolution fusion | flops 1076625408 | bytes 9441792 | tf_op jit(solution)/shard_map/dot_general | solution.py:23
  174.4 0.1 multiply_reduce_fusion.4
  174.6 5.9 %fusion.44 = f32[128,1024]{1,0:T(8,128)} fusion(bf16[4,2048,1024]{2,1,0:T(8,128)(2,1)} %refs_7_.1, bf16[4,1024,2048]{2,1,0:T(8,128)(2,1)} %refs_6_.1, f32[64,1024]{1,0:T(8,128)S(1)} %get-tuple-element.29, f32[64,1024]{1,0:T(8,128)S(1)} %get-tuple-element.26, f32[1024]{0:T(1024)S(1)} %bitcast.269, f32[128]{0:T(128)S(1)} %add_rsqrt_fusion.4), kind=kOutput, calls=%fused_computation.44 | convolution fusion | flops 1076625408 | bytes 9441792 | tf_op jit(solution)/shard_map/dot_general | solution.py:23
  180.4 1.7 fusion.361
  182.1 1.2 maximum_select_fusion.1
  183.3 1.2 maximum_select_fusion
  (21 shorter events, 0.2 us)
Async XLA Ops:
  8.0 30.6 %copy-start = (f32[64,1024]{1,0:T(8,128)S(1)}, f32[64,1024]{1,0:T(8,128)}, u32[]{:S(2)}) copy-start(f32[64,1024]{1,0:T(8,128)} %refs_0_.1) | copy-start | bytes 786436
  24.0 7.1 %collective-permute-start = (f32[64,1024]{1,0:T(8,128)S(1)}, f32[64,1024]{1,0:T(8,128)S(1)}, u32[]{:S(2)}, u32[]{:S(2)}) collective-permute-start(f32[64,1024]{1,0:T(8,128)S(1)} %fusion.129), channel_id=1, source_target_pairs={{0,4},{4,8},{8,12},{12,16},{16,20},{20,24},{24,28},{1,5},{5,9},{9,... | collective-permute-start | bytes 786440 | tf_op jit(solution)/shard_map/ppermute | solution.py:14
  26.4 12.2 %collective-permute-start.1 = (f32[64,1024]{1,0:T(8,128)S(1)}, f32[64,1024]{1,0:T(8,128)S(1)}, u32[]{:S(2)}, u32[]{:S(2)}) collective-permute-start(f32[64,1024]{1,0:T(8,128)S(1)} %fusion.129), channel_id=1, source_target_pairs={{0,16},{4,20},{8,24},{12,28},{1,17},{5,21},{9,25},{13,29},{2,18},{... | collective-permute-start | bytes 786440 | tf_op jit(solution)/shard_map/ppermute | solution.py:14
  130.2 6.2 %collective-permute-start.2 = (f32[3,64,1024]{2,1,0:T(8,128)}, f32[3,64,1024]{2,1,0:T(8,128)S(1)}, u32[]{:S(2)}, u32[]{:S(2)}) collective-permute-start(f32[3,64,1024]{2,1,0:T(8,128)} %pad_maximum_fusion.2), channel_id=1, source_target_pairs={{0,4},{4,8},{8,12},{12,16},{16,20},{20,24},{24,28},{1,5},{5,9},{9,... | collective-permute-start | bytes 2359304 | tf_op jit(solution)/shard_map/ppermute | solution.py:14
  132.3 27.5 %collective-permute-start.3 = (f32[3,64,1024]{2,1,0:T(8,128)}, f32[3,64,1024]{2,1,0:T(8,128)S(1)}, u32[]{:S(2)}, u32[]{:S(2)}) collective-permute-start(f32[3,64,1024]{2,1,0:T(8,128)} %pad_maximum_fusion.2), channel_id=1, source_target_pairs={{0,16},{4,20},{8,24},{12,28},{1,17},{5,21},{9,25},{13,29},{2,18},{... | collective-permute-start | bytes 2359304 | tf_op jit(solution)/shard_map/ppermute | solution.py:14
  137.2 23.3 %copy-start.1 = (f32[64,1024]{1,0:T(8,128)}, f32[64,1024]{1,0:T(8,128)S(1)}, u32[]{:S(2)}) copy-start(f32[64,1024]{1,0:T(8,128)S(1)} %get-tuple-element.28) | copy-start | bytes 786436
  160.5 0.7 copy-start.2
